TPU v7x, 32 devices: a whole 2x2x4 slice. The times are simulated.
32 devices in a mesh: gx: 4 (over x, core), gy: 8 (over z, y).
Axes of the slice: x: 2, y: 2, z: 4, core: 2. Of those that a mesh axis runs over, the one named last changes fastest.
Arguments:
- activations: bfloat16 [4096, 8192], P('gx', 'gy'), may hold values from -12 to 12
- out_grads: bfloat16 [4096, 4096], P('gx', 'gy'), may hold values from -12 to 12
- left_roots: float32 [32, 1024, 1024], P(('gx', 'gy')), may hold values from -20 to 20, as said below
- right_roots: float32 [32, 1024, 1024], P(('gx', 'gy')), may hold values from -20 to 20, as said below
Outputs:
- update: bfloat16 [8192, 4096], P(None, 'gy')
Inputs may be any that keep to these rules, and one draw needn't show every extreme that they name: `left_roots`: each block is symmetric positive definite. `right_roots`: each block is symmetric positive definite.
All inputs are finite; a program needn't handle non-finite values.
Results may differ from a plain program's by a relative error of at most 0.001.
Values may be sent and summed in bfloat16 or wider, within the bound.
No kernel may reach another device: no remote copies, remote signals or barrier semaphores. Data moves between devices by JAX's collectives and lax.ppermute only.
A program may use at most 128 MiB of HBM per device.

v0:
```python
import jax
import jax.numpy as jnp
from jax import lax
from jax.sharding import PartitionSpec as P


epsilon = 1e-06
AXES = ("gx", "gy")
PARTS = (1, 1)


def partner(block, axis, distance):
    count = lax.axis_size(axis)
    route = []
    for low in range(count):
        high = low | 1 << distance
        if high != low and high < count:
            route += [(low, high), (high, low)]
    return lax.ppermute(block, axis, route)


def general(activations, out_grads, left_roots, right_roots):
    block_size = left_roots.shape[1]
    half_width = block_size // 2
    parity = lax.axis_index("gy") % 2
    is_even = parity == 0
    gathered = lax.all_gather(activations, "gy", axis=1, tiled=True)
    summed = lax.psum_scatter(
        lax.dot_general(
            gathered, out_grads, (((0,), (0,)), ((), ())), preferred_element_type=jnp.float32
        ),
        "gx",
        scatter_dimension=0,
        tiled=True,
    )
    own_part = lax.dynamic_slice_in_dim(summed, parity * block_size, block_size, 0)
    far_part = lax.dynamic_slice_in_dim(summed, (1 - parity) * block_size, block_size, 0)
    received = partner(far_part, "gy", 0)
    left_block = jnp.where(is_even, own_part, received)
    right_block = jnp.where(is_even, received, own_part)
    grad_block = jnp.concatenate([left_block, right_block], axis=1)
    finished = precondition(grad_block, left_roots[0], right_roots[0])
    own_part = lax.dynamic_slice_in_dim(finished, parity * half_width, half_width, 1)
    far_part = lax.dynamic_slice_in_dim(finished, (1 - parity) * half_width, half_width, 1)
    received = partner(far_part, "gy", 0)
    upper_rows = jnp.where(is_even, own_part, received)
    lower_rows = jnp.where(is_even, received, own_part)
    paired = jnp.concatenate([upper_rows, lower_rows], axis=0)
    return lax.all_gather(paired, "gx", axis=0, tiled=True)


def precondition(grad_block, left_root, right_root):
    shaped = jnp.dot(
        jnp.dot(left_root, grad_block, precision=lax.Precision.HIGH),
        right_root,
        precision=lax.Precision.HIGH,
    )
    graft = jnp.sqrt(jnp.mean(grad_block * grad_block) + epsilon) / jnp.sqrt(
        jnp.mean(shaped * shaped) + epsilon
    )
    return (shaped * graft).astype(jnp.bfloat16)


def routes(n_gx, n_gy, target):
    found = []
    for gx in range(n_gx):
        for gy in range(n_gy):
            to = target(gx // 2, gx % 2, gy // 2, gy % 2)
            if to is not None:
                x, core, z, y = to
                found.append((gx * n_gy + gy, (2 * x + core) * n_gy + 2 * z + y))
    return found


def send(block, route):
    return lax.ppermute(block, AXES, route)


def chosen(table, z):
    value = jnp.int32(table[0])
    for position in range(1, len(table)):
        value = jnp.where(z == position, jnp.int32(table[position]), value)
    return value


def lined(activations, out_grads, left_roots, right_roots):
    n_gx, n_gy = lax.axis_size("gx"), lax.axis_size("gy")
    n_z = n_gy // 2
    gx, gy = lax.axis_index("gx"), lax.axis_index("gy")
    x, core, z, y = gx // 2, gx % 2, gy // 2, gy % 2
    block_size = left_roots.shape[1]
    half = block_size // 2
    widths = [half * part // sum(PARTS) for part in PARTS]
    starts = [sum(widths[:h]) for h in range(len(widths))]
    pieces = range(len(widths))
    left_root, right_root = left_roots[0], right_roots[0]

    def route(target):
        return routes(n_gx, n_gy, target)

    across_x = route(lambda x, c, z, y: (1 - x, c, z, y))
    across_y = route(lambda x, c, z, y: (x, c, z, 1 - y))
    across_xy = route(lambda x, c, z, y: (1 - x, c, z, 1 - y))
    across_cores = route(lambda x, c, z, y: (x, 1 - c, z, y))

    def moved(block, path):
        return send(block, path)

    own = []
    for h in pieces:
        near = lax.dynamic_slice_in_dim(activations, core * half + starts[h], widths[h], 1)
        far = lax.dynamic_slice_in_dim(
            activations, (1 - core) * half + starts[h], widths[h], 1
        )
        swapped = moved(far, across_cores)
        own.append(jnp.concatenate([near, swapped], axis=0))

    up_1 = route(lambda x, c, z, y: (x, c, z + 1, y) if z < n_z - 1 else None)
    down_1 = route(lambda x, c, z, y: (x, c, z - 1, y) if z > 0 else None)
    up_2 = route(lambda x, c, z, y: (x, c, z + 1, y) if 0 < z < n_z - 1 else None)
    down_2 = route(lambda x, c, z, y: (x, c, z - 1, y) if 0 < z < n_z - 1 else None)
    ends = route(
        lambda x, c, z, y: (x, c, z + 1, y) if z == n_z - 2 else ((x, c, z - 1, y) if z == 1 else None)
    )
    is_upper = z >= n_z // 2
    is_end = (z == 0) | (z == n_z - 1)
    first_up = [moved(own[h], up_1) for h in pieces]
    first_down = [moved(own[h], down_1) for h in pieces]
    second_up = [moved(first_up[h], up_2) for h in pieces]
    second_down = [moved(first_down[h], down_2) for h in pieces]
    second = [jnp.where(is_upper, u, d) for u, d in zip(second_up, second_down)]
    third = [moved(second[h], ends) for h in pieces]

    other_half = moved(out_grads, across_y)
    columns = jnp.where(
        y == 0,
        jnp.concatenate([out_grads, other_half], axis=1),
        jnp.concatenate([other_half, out_grads], axis=1),
    )
    columns = jnp.concatenate([columns, moved(columns, across_cores)], axis=0)

    def arrived(step, h):
        if step == 0:
            return own[h]
        if step == 1:
            return jnp.where(is_upper, first_up[h], first_down[h])
        if step == 2:
            opposite = jnp.where(is_upper, first_down[h], first_up[h])
            return jnp.where(is_end, second[h], opposite)
        return jnp.where(is_end, third[h], second[h])

    def partial_sum(step, h):
        return lax.dot_general(
            arrived(step, h),
            columns,
            (((0,), (0,)), ((), ())),
            preferred_element_type=jnp.float32,
        )

    tables = [[0, 1, 2, 3], [1, 2, 1, 2], [2, 0, 3, 1], [3, 3, 0, 0]]
    sources = [chosen(table, z) for table in tables]
    final = tables[-1]
    same_core = route(
        lambda x, c, z, y: (1 - x, c, z, y)
        if (x, c) == (1 - final[z] // 2, final[z] % 2)
        else None
    )
    cross_core = route(
        lambda x, c, z, y: (1 - x, 1 - c, z, y)
        if (x, c) == (1 - final[z] // 2, 1 - final[z] % 2)
        else None
    )
    chip_mate = route(
        lambda x, c, z, y: (x, 1 - c, z, y)
        if (x, c) == (final[z] // 2, 1 - final[z] % 2)
        else None
    )
    shaped = None
    squares = jnp.float32(0)
    for h in pieces:
        mine = theirs = None
        for step in range(3):
            part = partial_sum(step, h)
            table = tables[step]

            def to_owner(x, c, z, y):
                owner = table[z] // 2
                return (owner, c, z, y) if x != owner else None

            crossed = moved(part, route(to_owner))
            total = part + crossed
            if mine is None:
                mine, theirs = total, total
            else:
                mine = jnp.where(sources[step] == gx, total, mine)
                theirs = jnp.where(sources[step] == 2 * x + 1 - core, total, theirs)
        mine, theirs = lax.optimization_barrier((mine, theirs))
        theirs = moved(theirs, across_cores)
        part = partial_sum(3, h)
        from_same = moved(part, same_core)
        from_cross = moved(part, cross_core)
        from_mate = moved(part, chip_mate)
        low, high = starts[h], starts[h] + widths[h]
        weights = jnp.concatenate(
            [left_root[:, low:high], left_root[:, half + low : half + high]], axis=1
        )
        is_last = sources[3] == gx
        mine = jnp.where(is_last, part + from_same, mine)
        theirs = jnp.where(is_last, from_cross + from_mate, theirs)
        rows = jnp.concatenate(
            [jnp.where(core == 0, mine, theirs), jnp.where(core == 0, theirs, mine)], axis=0
        )
        squares = squares + jnp.sum(rows * rows)
        term = jnp.dot(
            weights,
            jnp.dot(rows, right_root, precision=lax.Precision.HIGH),
            precision=lax.Precision.HIGH,
        )
        shaped = term if shaped is None else shaped + term
    count = block_size * block_size
    graft = jnp.sqrt(squares / count + epsilon) / jnp.sqrt(jnp.mean(shaped * shaped) + epsilon)
    finished = (shaped * graft).astype(jnp.bfloat16)

    near = lax.dynamic_slice_in_dim(finished, y * half, half, 1)
    far = lax.dynamic_slice_in_dim(finished, (1 - y) * half, half, 1)
    far_parts = [far[:half], far[half:]]
    across = moved(near, across_x)
    beside = [moved(part, across_y) for part in far_parts]
    diagonal = [moved(part, across_x) for part in beside]
    depth = block_size // 2
    parts = [
        (near, x, y, 0),
        (beside[0], x, 1 - y, 0),
        (beside[1], x, 1 - y, depth),
        (across, 1 - x, y, 0),
        (diagonal[0], 1 - x, 1 - y, 0),
        (diagonal[1], 1 - x, 1 - y, depth),
    ]
    result = jnp.zeros((n_gx * 2 * block_size, half), jnp.bfloat16)
    for part, from_x, from_y, offset in parts:
        other = moved(part, across_cores)
        for block, from_core in ((part, core), (other, 1 - core)):
            row = (4 * from_x + 2 * from_core + from_y) * block_size + offset
            result = lax.dynamic_update_slice(result, block, (row, jnp.int32(0)))
    return result


def solution(mesh):
    in_specs = (
        P("gx", "gy"),
        P("gx", "gy"),
        P(("gx", "gy"), None, None),
        P(("gx", "gy"), None, None),
    )
    out_specs = P(None, "gy")

    n_gx, n_gy = mesh.shape["gx"], mesh.shape["gy"]
    paired = n_gx == 4 and n_gy == 2 * n_gx

    def local(activations, out_grads, left_roots, right_roots):
        if paired and activations.shape[1] == left_roots.shape[1]:
            return lined(activations, out_grads, left_roots, right_roots)
        return general(activations, out_grads, left_roots, right_roots)

    return jax.shard_map(local, mesh=mesh, in_specs=in_specs, out_specs=out_specs, check_vma=False)
```

profile of v0, /device:TPU:0, one launch (start us, length us, event | category | flops | bytes accessed | tf_op | source)
XLA Modules:
  0.0 331.8 jit_solution(2710305709493237773)
XLA Ops:
  0.0 1.8 constant_dynamic-slice_fusion.3
  3.9 5.8 %collective-permute-start.16 = (bf16[2048,256]{1,0:T(8,128)(2,1)S(1)}, bf16[2048,256]{1,0:T(8,128)(2,1)}, u32[]{:S(2)}, u32[]{:S(2)}) collective-permute-start(bf16[2048,256]{1,0:T(8,128)(2,1)S(1)} %pad_maximum_fusion.6), channel_id=1, source_target_pairs={{0,2},{1,3},{2,4},{3,5},{4,6},{5,7},{8,10},{9,11},{10,12},{11,13},... | collective-permute-start | bytes 3145736 | tf_op jit(solution)/shard_map/ppermute | solution.py:76
  11.1 1.6 collective-permute-start.6
  14.5 5.5 %collective-permute-start.1 = (bf16[2048,256]{1,0:T(8,128)(2,1)}, bf16[2048,256]{1,0:T(8,128)(2,1)}, u32[]{:S(2)}, u32[]{:S(2)}) collective-permute-start(bf16[2048,256]{1,0:T(8,128)(2,1)} %pad_maximum_fusion.5), channel_id=1, source_target_pairs={{0,2},{1,3},{2,4},{3,5},{4,6},{5,7},{8,10},{9,11},{10,12},{11,13},... | collective-permute-start | bytes 3145736 | tf_op jit(solution)/shard_map/ppermute | solution.py:76
  21.3 11.0 %collective-permute-done.16 = bf16[2048,256]{1,0:T(8,128)(2,1)} collective-permute-done((bf16[2048,256]{1,0:T(8,128)(2,1)S(1)}, bf16[2048,256]{1,0:T(8,128)(2,1)}, u32[]{:S(2)}, u32[]{:S(2)}) %collective-permute-start.16) | collective-permute-done | bytes 1048608 | tf_op jit(solution)/shard_map/ppermute | solution.py:76
  32.3 1.6 collective-permute-start.17
  34.0 3.8 %collective-permute-done.18 = bf16[2048,256]{1,0:T(8,128)(2,1)} collective-permute-done((bf16[2048,256]{1,0:T(8,128)(2,1)S(1)}, bf16[2048,256]{1,0:T(8,128)(2,1)}, u32[]{:S(2)}, u32[]{:S(2)}) %collective-permute-start.18) | collective-permute-done | bytes 1048608 | tf_op jit(solution)/shard_map/ppermute | solution.py:76
  39.1 3.1 maximum_select_fusion
  42.3 11.8 %collective-permute-done.1 = bf16[2048,256]{1,0:T(8,128)(2,1)} collective-permute-done((bf16[2048,256]{1,0:T(8,128)(2,1)}, bf16[2048,256]{1,0:T(8,128)(2,1)}, u32[]{:S(2)}, u32[]{:S(2)}) %collective-permute-start.1) | collective-permute-done | bytes 1048608 | tf_op jit(solution)/shard_map/ppermute | solution.py:76
  54.1 1.6 collective-permute-start.2
  55.7 4.6 %collective-permute-done.3 = bf16[2048,256]{1,0:T(8,128)(2,1)} collective-permute-done((bf16[2048,256]{1,0:T(8,128)(2,1)}, bf16[2048,256]{1,0:T(8,128)(2,1)}, u32[]{:S(2)}, u32[]{:S(2)}) %collective-permute-start.3) | collective-permute-done | bytes 1048608 | tf_op jit(solution)/shard_map/ppermute | solution.py:76
  61.6 21.1 %collective-permute-done.19 = bf16[2048,256]{1,0:T(8,128)(2,1)} collective-permute-done((bf16[2048,256]{1,0:T(8,128)(2,1)}, bf16[2048,256]{1,0:T(8,128)(2,1)}, u32[]{:S(2)}, u32[]{:S(2)}) %collective-permute-start.19) | collective-permute-done | bytes 1048608 | tf_op jit(solution)/shard_map/ppermute | solution.py:76
  85.4 19.8 %collective-permute-done.4 = bf16[2048,256]{1,0:T(8,128)(2,1)} collective-permute-done((bf16[2048,256]{1,0:T(8,128)(2,1)}, bf16[2048,256]{1,0:T(8,128)(2,1)}, u32[]{:S(2)}, u32[]{:S(2)}) %collective-permute-start.4) | collective-permute-done | bytes 1048608 | tf_op jit(solution)/shard_map/ppermute | solution.py:76
  107.8 3.2 fusion.13
  111.1 3.6 %collective-permute-start.22 = (f32[256,1024]{1,0:T(8,128)S(1)}, f32[256,1024]{1,0:T(8,128)S(1)}, u32[]{:S(2)}, u32[]{:S(2)}) collective-permute-start(f32[256,1024]{1,0:T(8,128)S(1)} %fusion.13), channel_id=1, source_target_pairs={{0,16},{1,17},{4,20},{5,21},{8,24},{9,25},{12,28},{13,29},{18,2},{... | collective-permute-start | bytes 3145736 | tf_op jit(solution)/shard_map/ppermute | solution.py:76
  114.7 3.2 fusion.11
  119.2 2.9 fusion.37
  123.4 3.2 fusion.20
  127.6 3.9 %collective-permute-start.9 = (f32[256,1024]{1,0:T(8,128)S(1)}, f32[256,1024]{1,0:T(8,128)S(1)}, u32[]{:S(2)}, u32[]{:S(2)}) collective-permute-start(f32[256,1024]{1,0:T(8,128)S(1)} %fusion.20), channel_id=1, source_target_pairs={{0,16},{1,17},{4,20},{5,21},{8,24},{9,25},{12,28},{13,29},{18,2},{... | collective-permute-start | bytes 3145736 | tf_op jit(solution)/shard_map/ppermute | solution.py:76
  131.5 3.2 fusion.18
  134.7 14.2 %collective-permute-done.5 = bf16[2048,256]{1,0:T(8,128)(2,1)S(1)} collective-permute-done((bf16[2048,256]{1,0:T(8,128)(2,1)S(1)}, bf16[2048,256]{1,0:T(8,128)(2,1)S(1)}, u32[]{:S(2)}, u32[]{:S(2)}) %collective-permute-start.5) | collective-permute-done | bytes 1048608 | tf_op jit(solution)/shard_map/ppermute | solution.py:76
  150.2 2.9 fusion.38
  154.4 2.9 fusion.16
  158.0 10.3 %collective-permute-done.24 = f32[256,1024]{1,0:T(8,128)S(1)} collective-permute-done((f32[256,1024]{1,0:T(8,128)S(1)}, f32[256,1024]{1,0:T(8,128)S(1)}, u32[]{:S(2)}, u32[]{:S(2)}) %collective-permute-start.24) | collective-permute-done | bytes 1048608 | tf_op jit(solution)/shard_map/ppermute | solution.py:76
  171.5 19.3 %collective-permute-done.10 = f32[256,1024]{1,0:T(8,128)S(1)} collective-permute-done((f32[256,1024]{1,0:T(8,128)S(1)}, f32[256,1024]{1,0:T(8,128)S(1)}, u32[]{:S(2)}, u32[]{:S(2)}) %collective-permute-start.10) | collective-permute-done | bytes 1048608 | tf_op jit(solution)/shard_map/ppermute | solution.py:76
  190.8 2.9 fusion.23
  193.6 16.2 %collective-permute-done.11 = f32[256,1024]{1,0:T(8,128)S(1)} collective-permute-done((f32[256,1024]{1,0:T(8,128)S(1)}, f32[256,1024]{1,0:T(8,128)S(1)}, u32[]{:S(2)}, u32[]{:S(2)}) %collective-permute-start.11) | collective-permute-done | bytes 1048608 | tf_op jit(solution)/shard_map/ppermute | solution.py:76
  213.6 1.8 fusion.39
  216.6 17.4 %collective-permute-done.12 = f32[256,1024]{1,0:T(8,128)S(1)} collective-permute-done((f32[256,1024]{1,0:T(8,128)S(1)}, f32[256,1024]{1,0:T(8,128)S(1)}, u32[]{:S(2)}, u32[]{:S(2)}) %collective-permute-start.12) | collective-permute-done | bytes 1048608 | tf_op jit(solution)/shard_map/ppermute | solution.py:76
  235.3 3.6 %fusion = f32[512,1024]{1,0:T(8,128)S(1)} fusion(f32[1,1024,1024]{2,1,0:T(8,128)S(1)} %copy-done, f32[256,1024]{1,0:T(8,128)S(1)} %broadcast_select_fusion.2, f32[256,1024]{1,0:T(8,128)S(1)} %get-tuple-element.15), kind=kOutput, calls=%fused_computation.1 | convolution fusion | flops 3221749760 | bytes 8388608 | tf_op jit(solution)/shard_map/dot_general | solution.py:216
  240.0 4.9 %fusion.2 = f32[512,1024]{1,0:T(8,128)} fusion(f32[1,1024,1024]{2,1,0:T(8,128)S(1)} %copy-done, f32[256,1024]{1,0:T(8,128)S(1)} %broadcast_select_fusion.4, f32[256,1024]{1,0:T(8,128)S(1)} %get-tuple-element.18), kind=kOutput, calls=%fused_computation.3 | convolution fusion | flops 3221749760 | bytes 8388608 | tf_op jit(solution)/shard_map/dot_general | solution.py:216
  246.2 6.0 %fusion.4 = f32[1024,1024]{1,0:T(8,128)S(1)} fusion(f32[512,1024]{1,0:T(8,128)} %fusion.2, f32[1024,256]{1,0:T(8,128)} %get-tuple-element.27, f32[1024,256]{1,0:T(8,128)} %get-tuple-element.28), kind=kOutput, calls=%fused_computation.8 | convolution fusion | flops 3221749760 | bytes 8388608 | tf_op jit(solution)/shard_map/dot_general | solution.py:214
  252.2 5.8 %multiply_reduce_fusion = (f32[]{:T(128)}, f32[1024,1024]{1,0:T(8,128)}) fusion(f32[1024,1024]{1,0:T(8,128)S(1)} %fusion.4, f32[512,1024]{1,0:T(8,128)S(1)} %fusion, f32[1024,256]{1,0:T(8,128)S(1)} %copy-done.2, f32[1024,256]{1,0:T(8,128)S(1)} %get-tuple-element.25), kind=kOutput, calls=%fused_computation.6 | convolution fusion | flops 3224895488 | bytes 12582916 | tf_op jit(solution)/shard_map/dot_general | solution.py:214
  258.7 2.8 multiply_convert_fusion
  261.5 3.9 %broadcast_in_dim.3 = bf16[8192,512]{1,0:T(8,128)(2,1)} broadcast(bf16[]{:T(256)} %constant.57.clone.1), dimensions={} | broadcast | bytes 8388610 | tf_op jit(solution)/shard_map/broadcast_in_dim | solution.py:239
  267.0 1.6 collective-permute-start.29
  270.5 10.4 %collective-permute-done.29 = bf16[512,512]{1,0:T(8,128)(2,1)} collective-permute-done((bf16[512,512]{1,0:T(8,128)(2,1)S(1)}, bf16[512,512]{1,0:T(8,128)(2,1)}, u32[]{:S(2)}, u32[]{:S(2)}) %collective-permute-start.29) | collective-permute-done | bytes 524320 | tf_op jit(solution)/shard_map/ppermute | solution.py:76
  280.9 3.1 collective-permute-start.35
  284.0 8.2 %collective-permute-done.31 = bf16[512,512]{1,0:T(8,128)(2,1)} collective-permute-done((bf16[512,512]{1,0:T(8,128)(2,1)S(1)}, bf16[512,512]{1,0:T(8,128)(2,1)}, u32[]{:S(2)}, u32[]{:S(2)}) %collective-permute-start.31) | collective-permute-done | bytes 524320 | tf_op jit(solution)/shard_map/ppermute | solution.py:76
  292.1 2.4 collective-permute-start.37
  295.0 9.4 %collective-permute-done.35 = bf16[512,512]{1,0:T(8,128)(2,1)} collective-permute-done((bf16[512,512]{1,0:T(8,128)(2,1)}, bf16[512,512]{1,0:T(8,128)(2,1)}, u32[]{:S(2)}, u32[]{:S(2)}) %collective-permute-start.35) | collective-permute-done | bytes 524320 | tf_op jit(solution)/shard_map/ppermute | solution.py:76
  304.5 10.8 %collective-permute-done.37 = bf16[512,512]{1,0:T(8,128)(2,1)} collective-permute-done((bf16[512,512]{1,0:T(8,128)(2,1)}, bf16[512,512]{1,0:T(8,128)(2,1)}, u32[]{:S(2)}, u32[]{:S(2)}) %collective-permute-start.37) | collective-permute-done | bytes 524320 | tf_op jit(solution)/shard_map/ppermute | solution.py:76
  316.8 1.9 constant_dynamic-update-slice_fusion.9
  318.7 1.9 constant_dynamic-update-slice_fusion.8
  320.6 1.9 constant_dynamic-update-slice_fusion.7
  322.4 1.9 constant_dynamic-update-slice_fusion.6
  326.4 1.9 constant_dynamic-update-slice_fusion.3
  329.1 1.9 constant_dynamic-update-slice_fusion.1
  (87 shorter events, 41.2 us)
Async XLA Ops:
  0.0 11.1 %copy-start.3 = (bf16[1024,512]{1,0:T(8,128)(2,1)S(1)}, bf16[1024,512]{1,0:T(8,128)(2,1)}, u32[]{:S(2)}) copy-start(bf16[1024,512]{1,0:T(8,128)(2,1)} %param.5) | copy-start | bytes 3145732
  1.8 2.1 collective-permute-start.15
  2.3 10.3 %collective-permute-start = (bf16[1024,256]{1,0:T(8,128)(2,1)S(1)}, bf16[1024,256]{1,0:T(8,128)(2,1)S(1)}, u32[]{:S(2)}, u32[]{:S(2)}) collective-permute-start(bf16[1024,256]{1,0:T(8,128)(2,1)S(1)} %get-tuple-element.32), channel_id=1, source_target_pairs={{0,8},{1,9},{2,10},{3,11},{4,12},{5,13},{6,14},{7,15},{8,0},{9,1},... | collective-permute-start | bytes 1572872 | tf_op jit(solution)/shard_map/ppermute | solution.py:76
  3.9 10.6 %copy-start.6 = (bf16[1024,256]{1,0:T(8,128)(2,1)}, bf16[1024,256]{1,0:T(8,128)(2,1)S(1)}, u32[]{:S(2)}) copy-start(bf16[1024,256]{1,0:T(8,128)(2,1)S(1)} %collective-permute-done.15) | copy-start | bytes 1572868
  3.9 28.4 %collective-permute-start.16 = (bf16[2048,256]{1,0:T(8,128)(2,1)S(1)}, bf16[2048,256]{1,0:T(8,128)(2,1)}, u32[]{:S(2)}, u32[]{:S(2)}) collective-permute-start(bf16[2048,256]{1,0:T(8,128)(2,1)S(1)} %pad_maximum_fusion.6), channel_id=1, source_target_pairs={{0,2},{1,3},{2,4},{3,5},{4,6},{5,7},{8,10},{9,11},{10,12},{11,13},... | collective-permute-start | bytes 3145736 | tf_op jit(solution)/shard_map/ppermute | solution.py:76
  9.8 28.0 %collective-permute-start.18 = (bf16[2048,256]{1,0:T(8,128)(2,1)S(1)}, bf16[2048,256]{1,0:T(8,128)(2,1)}, u32[]{:S(2)}, u32[]{:S(2)}) collective-permute-start(bf16[2048,256]{1,0:T(8,128)(2,1)S(1)} %pad_maximum_fusion.6), channel_id=1, source_target_pairs={{2,0},{3,1},{4,2},{5,3},{6,4},{7,5},{10,8},{11,9},{12,10},{13,11},... | collective-permute-start | bytes 3145736 | tf_op jit(solution)/shard_map/ppermute | solution.py:76
  11.1 28.0 %collective-permute-start.6 = (bf16[1024,512]{1,0:T(8,128)(2,1)S(1)}, bf16[1024,512]{1,0:T(8,128)(2,1)}, u32[]{:S(2)}, u32[]{:S(2)}) collective-permute-start(bf16[1024,512]{1,0:T(8,128)(2,1)S(1)} %copy-done.3), channel_id=1, source_target_pairs={{0,1},{1,0},{2,3},{3,2},{4,5},{5,4},{6,7},{7,6},{8,9},{9,8},{10,11... | collective-permute-start | bytes 3145736 | tf_op jit(solution)/shard_map/ppermute | solution.py:76
  12.6 0.8 copy-start.4
  14.5 39.6 %collective-permute-start.1 = (bf16[2048,256]{1,0:T(8,128)(2,1)}, bf16[2048,256]{1,0:T(8,128)(2,1)}, u32[]{:S(2)}, u32[]{:S(2)}) collective-permute-start(bf16[2048,256]{1,0:T(8,128)(2,1)} %pad_maximum_fusion.5), channel_id=1, source_target_pairs={{0,2},{1,3},{2,4},{3,5},{4,6},{5,7},{8,10},{9,11},{10,12},{11,13},... | collective-permute-start | bytes 3145736 | tf_op jit(solution)/shard_map/ppermute | solution.py:76
  20.0 40.2 %collective-permute-start.3 = (bf16[2048,256]{1,0:T(8,128)(2,1)}, bf16[2048,256]{1,0:T(8,128)(2,1)}, u32[]{:S(2)}, u32[]{:S(2)}) collective-permute-start(bf16[2048,256]{1,0:T(8,128)(2,1)} %pad_maximum_fusion.5), channel_id=1, source_target_pairs={{2,0},{3,1},{4,2},{5,3},{6,4},{7,5},{10,8},{11,9},{12,10},{13,11},... | collective-permute-start | bytes 3145736 | tf_op jit(solution)/shard_map/ppermute | solution.py:76
  32.3 29.3 %collective-permute-start.17 = (bf16[2048,256]{1,0:T(8,128)(2,1)}, bf16[2048,256]{1,0:T(8,128)(2,1)}, u32[]{:S(2)}, u32[]{:S(2)}) collective-permute-start(bf16[2048,256]{1,0:T(8,128)(2,1)} %collective-permute-done.16), channel_id=1, source_target_pairs={{2,4},{3,5},{4,6},{5,7},{10,12},{11,13},{12,14},{13,15},{18,20},{1... | collective-permute-start | bytes 3145736 | tf_op jit(solution)/shard_map/ppermute | solution.py:76
  37.8 44.9 %collective-permute-start.19 = (bf16[2048,256]{1,0:T(8,128)(2,1)}, bf16[2048,256]{1,0:T(8,128)(2,1)}, u32[]{:S(2)}, u32[]{:S(2)}) collective-permute-start(bf16[2048,256]{1,0:T(8,128)(2,1)} %collective-permute-done.18), channel_id=1, source_target_pairs={{2,0},{3,1},{4,2},{5,3},{10,8},{11,9},{12,10},{13,11},{18,16},{19,... | collective-permute-start | bytes 3145736 | tf_op jit(solution)/shard_map/ppermute | solution.py:76
  42.2 65.6 %collective-permute-start.7 = (bf16[1024,1024]{1,0:T(8,128)(2,1)S(1)}, bf16[1024,1024]{1,0:T(8,128)(2,1)}, u32[]{:S(2)}, u32[]{:S(2)}) collective-permute-start(bf16[1024,1024]{1,0:T(8,128)(2,1)S(1)} %maximum_select_fusion), channel_id=1, source_target_pairs={{0,8},{1,9},{2,10},{3,11},{4,12},{5,13},{6,14},{7,15},{8,0},{9,1},... | collective-permute-start | bytes 6291464 | tf_op jit(solution)/shard_map/ppermute | solution.py:76
  54.1 31.3 %collective-permute-start.2 = (bf16[2048,256]{1,0:T(8,128)(2,1)}, bf16[2048,256]{1,0:T(8,128)(2,1)}, u32[]{:S(2)}, u32[]{:S(2)}) collective-permute-start(bf16[2048,256]{1,0:T(8,128)(2,1)} %collective-permute-done.1), channel_id=1, source_target_pairs={{2,4},{3,5},{4,6},{5,7},{10,12},{11,13},{12,14},{13,15},{18,20},{1... | collective-permute-start | bytes 3145736 | tf_op jit(solution)/shard_map/ppermute | solution.py:76
  60.3 44.9 %collective-permute-start.4 = (bf16[2048,256]{1,0:T(8,128)(2,1)}, bf16[2048,256]{1,0:T(8,128)(2,1)}, u32[]{:S(2)}, u32[]{:S(2)}) collective-permute-start(bf16[2048,256]{1,0:T(8,128)(2,1)} %collective-permute-done.3), channel_id=1, source_target_pairs={{2,0},{3,1},{4,2},{5,3},{10,8},{11,9},{12,10},{13,11},{18,16},{19,... | collective-permute-start | bytes 3145736 | tf_op jit(solution)/shard_map/ppermute | solution.py:76
  84.1 43.5 %collective-permute-start.20 = (bf16[2048,256]{1,0:T(8,128)(2,1)S(1)}, bf16[2048,256]{1,0:T(8,128)(2,1)S(1)}, u32[]{:S(2)}, u32[]{:S(2)}) collective-permute-start(bf16[2048,256]{1,0:T(8,128)(2,1)S(1)} %broadcast_select_fusion), channel_id=1, source_target_pairs={{2,0},{3,1},{4,6},{5,7},{10,8},{11,9},{12,14},{13,15},{18,16},{19,... | collective-permute-start | bytes 3145736 | tf_op jit(solution)/shard_map/ppermute | solution.py:76
  106.5 42.4 %collective-permute-start.5 = (bf16[2048,256]{1,0:T(8,128)(2,1)S(1)}, bf16[2048,256]{1,0:T(8,128)(2,1)S(1)}, u32[]{:S(2)}, u32[]{:S(2)}) collective-permute-start(bf16[2048,256]{1,0:T(8,128)(2,1)S(1)} %broadcast_select_fusion.1), channel_id=1, source_target_pairs={{2,0},{3,1},{4,6},{5,7},{10,8},{11,9},{12,14},{13,15},{18,16},{19,... | collective-permute-start | bytes 3145736 | tf_op jit(solution)/shard_map/ppermute | solution.py:76
  111.1 8.1 %copy-start.7 = (bf16[1024,256]{1,0:T(8,128)(2,1)S(1)}, bf16[1024,256]{1,0:T(8,128)(2,1)}, u32[]{:S(2)}) copy-start(bf16[1024,256]{1,0:T(8,128)(2,1)} %copy-done.6) | copy-start | bytes 1572868
  111.1 42.0 %collective-permute-start.22 = (f32[256,1024]{1,0:T(8,128)S(1)}, f32[256,1024]{1,0:T(8,128)S(1)}, u32[]{:S(2)}, u32[]{:S(2)}) collective-permute-start(f32[256,1024]{1,0:T(8,128)S(1)} %fusion.13), channel_id=1, source_target_pairs={{0,16},{1,17},{4,20},{5,21},{8,24},{9,25},{12,28},{13,29},{18,2},{... | collective-permute-start | bytes 3145736 | tf_op jit(solution)/shard_map/ppermute | solution.py:76
  117.9 39.4 %collective-permute-start.23 = (f32[256,1024]{1,0:T(8,128)S(1)}, f32[256,1024]{1,0:T(8,128)S(1)}, u32[]{:S(2)}, u32[]{:S(2)}) collective-permute-start(f32[256,1024]{1,0:T(8,128)S(1)} %fusion.11), channel_id=1, source_target_pairs={{2,18},{3,19},{6,22},{7,23},{10,26},{11,27},{14,30},{15,31},{16,0}... | collective-permute-start | bytes 3145736 | tf_op jit(solution)/shard_map/ppermute | solution.py:76
  122.1 46.2 %collective-permute-start.24 = (f32[256,1024]{1,0:T(8,128)S(1)}, f32[256,1024]{1,0:T(8,128)S(1)}, u32[]{:S(2)}, u32[]{:S(2)}) collective-permute-start(f32[256,1024]{1,0:T(8,128)S(1)} %fusion.37), channel_id=1, source_target_pairs={{4,20},{5,21},{6,22},{7,23},{12,28},{13,29},{14,30},{15,31},{16,0}... | collective-permute-start | bytes 3145736 | tf_op jit(solution)/shard_map/ppermute | solution.py:76
  126.6 23.6 %copy-start.5 = (bf16[1024,256]{1,0:T(8,128)(2,1)S(1)}, bf16[1024,256]{1,0:T(8,128)(2,1)}, u32[]{:S(2)}) copy-start(bf16[1024,256]{1,0:T(8,128)(2,1)} %copy-done.4) | copy-start | bytes 1572868
  127.6 42.1 %collective-permute-start.9 = (f32[256,1024]{1,0:T(8,128)S(1)}, f32[256,1024]{1,0:T(8,128)S(1)}, u32[]{:S(2)}, u32[]{:S(2)}) collective-permute-start(f32[256,1024]{1,0:T(8,128)S(1)} %fusion.20), channel_id=1, source_target_pairs={{0,16},{1,17},{4,20},{5,21},{8,24},{9,25},{12,28},{13,29},{18,2},{... | collective-permute-start | bytes 3145736 | tf_op jit(solution)/shard_map/ppermute | solution.py:76
  148.9 41.8 %collective-permute-start.10 = (f32[256,1024]{1,0:T(8,128)S(1)}, f32[256,1024]{1,0:T(8,128)S(1)}, u32[]{:S(2)}, u32[]{:S(2)}) collective-permute-start(f32[256,1024]{1,0:T(8,128)S(1)} %fusion.18), channel_id=1, source_target_pairs={{2,18},{3,19},{6,22},{7,23},{10,26},{11,27},{14,30},{15,31},{16,0}... | collective-permute-start | bytes 3145736 | tf_op jit(solution)/shard_map/ppermute | solution.py:76
  153.1 56.8 %collective-permute-start.11 = (f32[256,1024]{1,0:T(8,128)S(1)}, f32[256,1024]{1,0:T(8,128)S(1)}, u32[]{:S(2)}, u32[]{:S(2)}) collective-permute-start(f32[256,1024]{1,0:T(8,128)S(1)} %fusion.38), channel_id=1, source_target_pairs={{4,20},{5,21},{6,22},{7,23},{12,28},{13,29},{14,30},{15,31},{16,0}... | collective-permute-start | bytes 3145736 | tf_op jit(solution)/shard_map/ppermute | solution.py:76
  157.3 54.8 %collective-permute-start.21 = (f32[256,1024]{1,0:T(8,128)S(1)}, f32[256,1024]{1,0:T(8,128)S(1)}, u32[]{:S(2)}, u32[]{:S(2)}) collective-permute-start(f32[256,1024]{1,0:T(8,128)S(1)} %fusion.16), channel_id=1, source_target_pairs={{8,24},{9,25},{10,26},{11,27},{20,4},{21,5},{22,6},{23,7}} | collective-permute-start | bytes 3145736 | tf_op jit(solution)/shard_map/ppermute | solution.py:76
  168.3 44.5 %collective-permute-start.25 = (f32[256,1024]{1,0:T(8,128)S(1)}, f32[256,1024]{1,0:T(8,128)S(1)}, u32[]{:S(2)}, u32[]{:S(2)}) collective-permute-start(f32[256,1024]{1,0:T(8,128)S(1)} %fusion.16), channel_id=1, source_target_pairs={{0,24},{1,25},{2,26},{3,27},{28,4},{29,5},{30,6},{31,7}} | collective-permute-start | bytes 3145736 | tf_op jit(solution)/shard_map/ppermute | solution.py:76
  169.7 43.9 %collective-permute-start.26 = (f32[256,1024]{1,0:T(8,128)S(1)}, f32[256,1024]{1,0:T(8,128)S(1)}, u32[]{:S(2)}, u32[]{:S(2)}) collective-permute-start(f32[256,1024]{1,0:T(8,128)S(1)} %fusion.16), channel_id=1, source_target_pairs={{12,4},{13,5},{14,6},{15,7},{16,24},{17,25},{18,26},{19,27}} | collective-permute-start | bytes 3145736 | tf_op jit(solution)/shard_map/ppermute | solution.py:76
  190.8 24.6 %collective-permute-start.27 = (f32[256,1024]{1,0:T(8,128)S(1)}, f32[256,1024]{1,0:T(8,128)S(1)}, u32[]{:S(2)}, u32[]{:S(2)}) collective-permute-start(f32[256,1024]{1,0:T(8,128)S(1)} %get-tuple-element.12), channel_id=1, source_target_pairs={{0,8},{1,9},{2,10},{3,11},{4,12},{5,13},{6,14},{7,15},{8,0},{9,1},... | collective-permute-start | bytes 3145736 | tf_op jit(solution)/shard_map/ppermute | solution.py:76
  193.6 20.0 %copy-start.1 = (f32[1,1024,1024]{2,1,0:T(8,128)S(1)}, f32[1,1024,1024]{2,1,0:T(8,128)}, u32[]{:S(2)}) copy-start(f32[1,1024,1024]{2,1,0:T(8,128)} %param.6) | copy-start | bytes 12582916
  209.9 24.2 %collective-permute-start.12 = (f32[256,1024]{1,0:T(8,128)S(1)}, f32[256,1024]{1,0:T(8,128)S(1)}, u32[]{:S(2)}, u32[]{:S(2)}) collective-permute-start(f32[256,1024]{1,0:T(8,128)S(1)} %fusion.23), channel_id=1, source_target_pairs={{0,24},{1,25},{2,26},{3,27},{28,4},{29,5},{30,6},{31,7}} | collective-permute-start | bytes 3145736 | tf_op jit(solution)/shard_map/ppermute | solution.py:76
  212.1 22.0 %collective-permute-start.13 = (f32[256,1024]{1,0:T(8,128)S(1)}, f32[256,1024]{1,0:T(8,128)S(1)}, u32[]{:S(2)}, u32[]{:S(2)}) collective-permute-start(f32[256,1024]{1,0:T(8,128)S(1)} %fusion.23), channel_id=1, source_target_pairs={{12,4},{13,5},{14,6},{15,7},{16,24},{17,25},{18,26},{19,27}} | collective-permute-start | bytes 3145736 | tf_op jit(solution)/shard_map/ppermute | solution.py:76
  212.8 21.3 %collective-permute-start.8 = (f32[256,1024]{1,0:T(8,128)S(1)}, f32[256,1024]{1,0:T(8,128)S(1)}, u32[]{:S(2)}, u32[]{:S(2)}) collective-permute-start(f32[256,1024]{1,0:T(8,128)S(1)} %fusion.23), channel_id=1, source_target_pairs={{8,24},{9,25},{10,26},{11,27},{20,4},{21,5},{22,6},{23,7}} | collective-permute-start | bytes 3145736 | tf_op jit(solution)/shard_map/ppermute | solution.py:76
  213.5 20.5 %collective-permute-start.14 = (f32[256,1024]{1,0:T(8,128)S(1)}, f32[256,1024]{1,0:T(8,128)S(1)}, u32[]{:S(2)}, u32[]{:S(2)}) collective-permute-start(f32[256,1024]{1,0:T(8,128)S(1)} %get-tuple-element.10), channel_id=1, source_target_pairs={{0,8},{1,9},{2,10},{3,11},{4,12},{5,13},{6,14},{7,15},{8,0},{9,1},... | collective-permute-start | bytes 3145736 | tf_op jit(solution)/shard_map/ppermute | solution.py:76
  216.6 18.7 %copy-start = (f32[1,1024,1024]{2,1,0:T(8,128)S(1)}, f32[1,1024,1024]{2,1,0:T(8,128)}, u32[]{:S(2)}) copy-start(f32[1,1024,1024]{2,1,0:T(8,128)} %param.7) | copy-start | bytes 12582916
  246.2 6.0 %copy-start.2 = (f32[1024,256]{1,0:T(8,128)S(1)}, f32[1024,256]{1,0:T(8,128)}, u32[]{:S(2)}) copy-start(f32[1024,256]{1,0:T(8,128)} %get-tuple-element.26) | copy-start | bytes 3145732
  266.9 27.6 %collective-permute-start.33 = (bf16[1024,512]{1,0:T(8,128)(2,1)}, bf16[1024,512]{1,0:T(8,128)(2,1)S(1)}, u32[]{:S(2)}, u32[]{:S(2)}) collective-permute-start(bf16[1024,512]{1,0:T(8,128)(2,1)} %get-tuple-element.14), channel_id=1, source_target_pairs={{0,16},{1,17},{2,18},{3,19},{4,20},{5,21},{6,22},{7,23},{8,24},{9,... | collective-permute-start | bytes 3145736 | tf_op jit(solution)/shard_map/ppermute | solution.py:76
  267.0 13.9 %collective-permute-start.29 = (bf16[512,512]{1,0:T(8,128)(2,1)S(1)}, bf16[512,512]{1,0:T(8,128)(2,1)}, u32[]{:S(2)}, u32[]{:S(2)}) collective-permute-start(bf16[512,512]{1,0:T(8,128)(2,1)S(1)} %get-tuple-element.30), channel_id=1, source_target_pairs={{0,1},{1,0},{2,3},{3,2},{4,5},{5,4},{6,7},{7,6},{8,9},{9,8},{10,11... | collective-permute-start | bytes 1572872 | tf_op jit(solution)/shard_map/ppermute | solution.py:76
  268.6 23.6 %collective-permute-start.31 = (bf16[512,512]{1,0:T(8,128)(2,1)S(1)}, bf16[512,512]{1,0:T(8,128)(2,1)}, u32[]{:S(2)}, u32[]{:S(2)}) collective-permute-start(bf16[512,512]{1,0:T(8,128)(2,1)S(1)} %get-tuple-element.29), channel_id=1, source_target_pairs={{0,1},{1,0},{2,3},{3,2},{4,5},{5,4},{6,7},{7,6},{8,9},{9,8},{10,11... | collective-permute-start | bytes 1572872 | tf_op jit(solution)/shard_map/ppermute | solution.py:76
  269.1 46.2 %collective-permute-start.28 = (bf16[1024,512]{1,0:T(8,128)(2,1)}, bf16[1024,512]{1,0:T(8,128)(2,1)S(1)}, u32[]{:S(2)}, u32[]{:S(2)}) collective-permute-start(bf16[1024,512]{1,0:T(8,128)(2,1)} %get-tuple-element.14), channel_id=1, source_target_pairs={{0,8},{1,9},{2,10},{3,11},{4,12},{5,13},{6,14},{7,15},{8,0},{9,1},... | collective-permute-start | bytes 3145736 | tf_op jit(solution)/shard_map/ppermute | solution.py:76
  280.9 23.6 %collective-permute-start.35 = (bf16[512,512]{1,0:T(8,128)(2,1)}, bf16[512,512]{1,0:T(8,128)(2,1)}, u32[]{:S(2)}, u32[]{:S(2)}) collective-permute-start(bf16[512,512]{1,0:T(8,128)(2,1)} %collective-permute-done.29), channel_id=1, source_target_pairs={{0,16},{1,17},{2,18},{3,19},{4,20},{5,21},{6,22},{7,23},{8,24},{9,... | collective-permute-start | bytes 1572872 | tf_op jit(solution)/shard_map/ppermute | solution.py:76
  292.1 23.1 %collective-permute-start.37 = (bf16[512,512]{1,0:T(8,128)(2,1)}, bf16[512,512]{1,0:T(8,128)(2,1)}, u32[]{:S(2)}, u32[]{:S(2)}) collective-permute-start(bf16[512,512]{1,0:T(8,128)(2,1)} %collective-permute-done.31), channel_id=1, source_target_pairs={{0,16},{1,17},{2,18},{3,19},{4,20},{5,21},{6,22},{7,23},{8,24},{9,... | collective-permute-start | bytes 1572872 | tf_op jit(solution)/shard_map/ppermute | solution.py:76
  294.5 30.8 %collective-permute-start.34 = (bf16[1024,512]{1,0:T(8,128)(2,1)S(1)}, bf16[1024,512]{1,0:T(8,128)(2,1)S(1)}, u32[]{:S(2)}, u32[]{:S(2)}) collective-permute-start(bf16[1024,512]{1,0:T(8,128)(2,1)S(1)} %collective-permute-done.33), channel_id=1, source_target_pairs={{0,8},{1,9},{2,10},{3,11},{4,12},{5,13},{6,14},{7,15},{8,0},{9,1},... | collective-permute-start | bytes 3145736 | tf_op jit(solution)/shard_map/ppermute | solution.py:76
  294.5 24.2 %collective-permute-start.30 = (bf16[512,512]{1,0:T(8,128)(2,1)}, bf16[512,512]{1,0:T(8,128)(2,1)}, u32[]{:S(2)}, u32[]{:S(2)}) collective-permute-start(bf16[512,512]{1,0:T(8,128)(2,1)} %collective-permute-done.29), channel_id=1, source_target_pairs={{0,8},{1,9},{2,10},{3,11},{4,12},{5,13},{6,14},{7,15},{8,0},{9,1},... | collective-permute-start | bytes 1572872 | tf_op jit(solution)/shard_map/ppermute | solution.py:76
  304.4 18.0 %collective-permute-start.32 = (bf16[512,512]{1,0:T(8,128)(2,1)}, bf16[512,512]{1,0:T(8,128)(2,1)}, u32[]{:S(2)}, u32[]{:S(2)}) collective-permute-start(bf16[512,512]{1,0:T(8,128)(2,1)} %collective-permute-done.31), channel_id=1, source_target_pairs={{0,8},{1,9},{2,10},{3,11},{4,12},{5,13},{6,14},{7,15},{8,0},{9,1},... | collective-permute-start | bytes 1572872 | tf_op jit(solution)/shard_map/ppermute | solution.py:76
  315.3 13.0 %collective-permute-start.36 = (bf16[512,512]{1,0:T(8,128)(2,1)}, bf16[512,512]{1,0:T(8,128)(2,1)S(1)}, u32[]{:S(2)}, u32[]{:S(2)}) collective-permute-start(bf16[512,512]{1,0:T(8,128)(2,1)} %collective-permute-done.35), channel_id=1, source_target_pairs={{0,8},{1,9},{2,10},{3,11},{4,12},{5,13},{6,14},{7,15},{8,0},{9,1},... | collective-permute-start | bytes 1572872 | tf_op jit(solution)/shard_map/ppermute | solution.py:76
  315.3 15.7 %collective-permute-start.38 = (bf16[512,512]{1,0:T(8,128)(2,1)}, bf16[512,512]{1,0:T(8,128)(2,1)S(1)}, u32[]{:S(2)}, u32[]{:S(2)}) collective-permute-start(bf16[512,512]{1,0:T(8,128)(2,1)} %collective-permute-done.37), channel_id=1, source_target_pairs={{0,8},{1,9},{2,10},{3,11},{4,12},{5,13},{6,14},{7,15},{8,0},{9,1},... | collective-permute-start | bytes 1572872 | tf_op jit(solution)/shard_map/ppermute | solution.py:76
where the time goes:
time: 333 us; the launch traced here: 332 us
  waiting for transfers between devices  191 us (57%)
  starting transfers between devices  53.2 us (16%)
  matrix products  44.6 us (13%)
  local copies, waits for them, and re-layouts  25.9 us (8%)
  other arithmetic  15 us (5%)
    ppermute x39, waiting for transfers between devices, send(): return lax.ppermute(block, AXES, route)  191 us
    ppermute x39, starting transfers between devices, send(): return lax.ppermute(block, AXES, route)  53.2 us
    dot_general x8, matrix products, partial_sum(): lax.dot_general(arrived(step, h), columns, (((0,), (0,)), ((), ())), pref...  24.3 us
    dynamic_update_slice x12, local copies, waits for them, and re-layouts, lined(): result = lax.dynamic_update_slice(result, block, (row, jnp.int32(0)))  17.4 us
    dot_general x2, matrix products, lined(): jnp.dot(weights, jnp.dot(rows, right_root, precision=lax.Precision.HIGH),...  11.9 us
    dot_general x2, matrix products, lined(): jnp.dot(rows, right_root, precision=lax.Precision.HIGH)  8.42 us
  transfers between devices with their start and end apart: 39, of which 17 were waited for; matrix products, arithmetic and copies ran while one was open for 15% of the time, Pallas kernels for 0%

commit v1 on v0

--- a/solution.py
+++ b/solution.py
@@ -1,12 +1,15 @@
 import jax
 import jax.numpy as jnp
 from jax import lax
+from jax.experimental import pallas as pl
+from jax.experimental.pallas import tpu as pltpu
 from jax.sharding import PartitionSpec as P
 
 
 epsilon = 1e-06
 AXES = ("gx", "gy")
 PARTS = (1, 1)
+STRIPS = 4
 
 
 def partner(block, axis, distance):
@@ -76,6 +79,164 @@
     return lax.ppermute(block, AXES, route)
 
 
+def in_vmem(count):
+    return [pl.BlockSpec(memory_space=pltpu.VMEM)] * count
+
+
+def params(mebibytes):
+    return pltpu.CompilerParams(vmem_limit_bytes=mebibytes * 2**20)
+
+
+def whereabouts():
+    gx, gy = lax.axis_index("gx"), lax.axis_index("gy")
+    return gx // 2, gx % 2, gy // 2, gy % 2
+
+
+def transposed_product(choices, columns, pick):
+    contracted, width = choices[0].shape
+    count = columns.shape[1]
+
+    def kernel(*refs):
+        *choice_refs, columns_ref, out_ref, taken_ref = refs
+        if len(choice_refs) == 1:
+            taken_ref = choice_refs[0]
+        else:
+            index = pick(whereabouts()[2])
+
+            def take(choice_ref):
+                taken_ref[...] = choice_ref[...]
+
+            for number, choice_ref in enumerate(choice_refs):
+                pl.when(index == number)(lambda ref=choice_ref: take(ref))
+
+        out_ref[...] = lax.dot_general(
+            taken_ref[...],
+            columns_ref[...],
+            (((0,), (0,)), ((), ())),
+            preferred_element_type=jnp.float32,
+        )
+
+    return pl.pallas_call(
+        kernel,
+        out_shape=jax.ShapeDtypeStruct((width, count), jnp.float32),
+        in_specs=in_vmem(len(choices) + 1),
+        out_specs=in_vmem(1)[0],
+        scratch_shapes=[pltpu.VMEM((contracted, width), jnp.bfloat16)],
+        cost_estimate=pl.CostEstimate(
+            flops=2 * contracted * width * count,
+            transcendentals=0,
+            bytes_accessed=2 * contracted * (width + count) + 4 * width * count,
+        ),
+        compiler_params=params(16),
+        name="token_product",
+    )(*choices, columns)
+
+
+def halves(value):
+    high = value.astype(jnp.bfloat16)
+    return high, (value - high.astype(jnp.float32)).astype(jnp.bfloat16)
+
+
+def kept_halves(value):
+    high = lax.reduce_precision(value, exponent_bits=8, mantissa_bits=7)
+    return high.astype(jnp.bfloat16), (value - high).astype(jnp.bfloat16)
+
+
+def three_pass(left, right):
+    def single(a, b):
+        return jnp.dot(a, b, preferred_element_type=jnp.float32)
+
+    return single(left[0], right[0]) + (single(left[0], right[1]) + single(left[1], right[0]))
+
+
+def advance(squares, sums, left, right, so_far, final, low, last):
+    width = sums[0].shape[0]
+    size = right[0].shape[0]
+    half = size // 2
+    strip = size // STRIPS
+    given = 0 if so_far is None else 1
+
+    def kernel(*refs):
+        squares_ref, part, same, cross, mate, mine, theirs, lh, ll, rh, rl = refs[:11]
+        acc = refs[11] if given else None
+        outs, (shaped, rows) = refs[11 + given : -2], refs[-2:]
+        if not last:
+            shaped = outs[0]
+        x, core, z, y = whereabouts()
+        is_last = chosen(final, z) == 2 * x + core
+        my_rows = jnp.where(is_last, part[...] + same[...], mine[...])
+        their_rows = jnp.where(is_last, cross[...] + mate[...], theirs[...])
+        rows[:width] = jnp.where(core == 0, my_rows, their_rows)
+        rows[width:] = jnp.where(core == 0, their_rows, my_rows)
+        entry = squares_ref[0] + jnp.sum(my_rows * my_rows) + jnp.sum(their_rows * their_rows)
+        piece = halves(rows[...])
+
+        inner = halves(three_pass(piece, (rh[...], rl[...])))
+
+        def second(number, total):
+            at = pl.ds(pl.multiple_of(number * strip, strip), strip)
+
+            def weights(ref):
+                return jnp.concatenate(
+                    [ref[at, low : low + width], ref[at, half + low : half + low + width]], axis=1
+                )
+
+            block = three_pass((weights(lh), weights(ll)), inner)
+            if given:
+                block = acc[at] + block
+            shaped[at] = block
+            return total + jnp.sum(block * block) if last else total
+
+        result = lax.fori_loop(0, STRIPS, second, jnp.float32(0), unroll=True)
+        if not last:
+            outs[1][0] = entry
+            return
+        near, far_0, far_1 = outs
+        count = size * size
+        graft = jnp.sqrt(entry / count + epsilon) / jnp.sqrt(result / count + epsilon)
+
+        def store(near_columns, far_columns):
+            near[...] = (shaped[:, near_columns] * graft).astype(jnp.bfloat16)
+            far_0[...] = (shaped[:half, far_columns] * graft).astype(jnp.bfloat16)
+            far_1[...] = (shaped[half:, far_columns] * graft).astype(jnp.bfloat16)
+
+        one, other = pl.ds(0, half), pl.ds(half, half)
+        pl.when(y == 0)(lambda: store(one, other))
+        pl.when(y == 1)(lambda: store(other, one))
+
+    smem = pl.BlockSpec(memory_space=pltpu.SMEM)
+    if last:
+        out_shape = [
+            jax.ShapeDtypeStruct((size, half), jnp.bfloat16),
+            jax.ShapeDtypeStruct((half, half), jnp.bfloat16),
+            jax.ShapeDtypeStruct((half, half), jnp.bfloat16),
+        ]
+        out_specs = in_vmem(3)
+    else:
+        out_shape = [
+            jax.ShapeDtypeStruct((size, size), jnp.float32),
+            jax.ShapeDtypeStruct((1,), jnp.float32),
+        ]
+        out_specs = in_vmem(1) + [smem]
+    scratch_size = size if last else 8
+    return pl.pallas_call(
+        kernel,
+        out_shape=out_shape,
+        in_specs=[smem] + in_vmem(10 + given),
+        out_specs=out_specs,
+        input_output_aliases={11: 0} if given and not last else {},
+        scratch_shapes=[
+            pltpu.VMEM((scratch_size, size), jnp.float32),
+            pltpu.VMEM((2 * width, size), jnp.float32),
+        ],
+        cost_estimate=pl.CostEstimate(
+            flops=24 * width * size * size, transcendentals=0, bytes_accessed=20 * size * size
+        ),
+        compiler_params=params(24 if last else 16),
+        name="finish" if last else "advance",
+    )(squares, *sums, *left, *right, *([so_far] if given else []))
+
+
 def chosen(table, z):
     value = jnp.int32(table[0])
     for position in range(1, len(table)):
@@ -123,7 +284,6 @@
         lambda x, c, z, y: (x, c, z + 1, y) if z == n_z - 2 else ((x, c, z - 1, y) if z == 1 else None)
     )
     is_upper = z >= n_z // 2
-    is_end = (z == 0) | (z == n_z - 1)
     first_up = [moved(own[h], up_1) for h in pieces]
     first_down = [moved(own[h], down_1) for h in pieces]
     second_up = [moved(first_up[h], up_2) for h in pieces]
@@ -139,22 +299,27 @@
     )
     columns = jnp.concatenate([columns, moved(columns, across_cores)], axis=0)
 
-    def arrived(step, h):
+    def partial_sum(step, h):
+        def lower(z):
+            return z < n_z // 2
+
+        def at_end(z):
+            return (z == 0) | (z == n_z - 1)
+
         if step == 0:
-            return own[h]
+            return transposed_product([own[h]], columns, None)
         if step == 1:
-            return jnp.where(is_upper, first_up[h], first_down[h])
+            return transposed_product(
+                [first_up[h], first_down[h]], columns, lambda z: jnp.where(lower(z), 1, 0)
+            )
         if step == 2:
-            opposite = jnp.where(is_upper, first_down[h], first_up[h])
-            return jnp.where(is_end, second[h], opposite)
-        return jnp.where(is_end, third[h], second[h])
-
-    def partial_sum(step, h):
-        return lax.dot_general(
-            arrived(step, h),
-            columns,
-            (((0,), (0,)), ((), ())),
-            preferred_element_type=jnp.float32,
+            return transposed_product(
+                [second[h], first_up[h], first_down[h]],
+                columns,
+                lambda z: jnp.where(at_end(z), 0, jnp.where(lower(z), 1, 2)),
+            )
+        return transposed_product(
+            [third[h], second[h]], columns, lambda z: jnp.where(at_end(z), 0, 1)
         )
 
     tables = [[0, 1, 2, 3], [1, 2, 1, 2], [2, 0, 3, 1], [3, 3, 0, 0]]
@@ -176,7 +341,8 @@
         else None
     )
     shaped = None
-    squares = jnp.float32(0)
+    squares = jnp.zeros((1,), jnp.float32)
+    left, right = kept_halves(left_root), kept_halves(right_root)
     for h in pieces:
         mine = theirs = None
         for step in range(3):
@@ -200,30 +366,21 @@
         from_same = moved(part, same_core)
         from_cross = moved(part, cross_core)
         from_mate = moved(part, chip_mate)
-        low, high = starts[h], starts[h] + widths[h]
-        weights = jnp.concatenate(
-            [left_root[:, low:high], left_root[:, half + low : half + high]], axis=1
+        final_piece = h == len(widths) - 1
+        outcome = advance(
+            squares,
+            (part, from_same, from_cross, from_mate, mine, theirs),
+            left,
+            right,
+            shaped,
+            final,
+            starts[h],
+            final_piece,
         )
-        is_last = sources[3] == gx
-        mine = jnp.where(is_last, part + from_same, mine)
-        theirs = jnp.where(is_last, from_cross + from_mate, theirs)
-        rows = jnp.concatenate(
-            [jnp.where(core == 0, mine, theirs), jnp.where(core == 0, theirs, mine)], axis=0
-        )
-        squares = squares + jnp.sum(rows * rows)
-        term = jnp.dot(
-            weights,
-            jnp.dot(rows, right_root, precision=lax.Precision.HIGH),
-            precision=lax.Precision.HIGH,
-        )
-        shaped = term if shaped is None else shaped + term
-    count = block_size * block_size
-    graft = jnp.sqrt(squares / count + epsilon) / jnp.sqrt(jnp.mean(shaped * shaped) + epsilon)
-    finished = (shaped * graft).astype(jnp.bfloat16)
-
-    near = lax.dynamic_slice_in_dim(finished, y * half, half, 1)
-    far = lax.dynamic_slice_in_dim(finished, (1 - y) * half, half, 1)
-    far_parts = [far[:half], far[half:]]
+        if not final_piece:
+            shaped, squares = outcome
+    near, *far_parts = outcome
+
     across = moved(near, across_x)
     beside = [moved(part, across_y) for part in far_parts]
     diagonal = [moved(part, across_x) for part in beside]

time: 333 us -> 307 us (0.922)
  matrix products: 44.6 us -> 0 us
  Pallas kernels: 0 us -> 37.1 us
  waiting for transfers between devices: 191 us -> 181 us
  local copies, waits for them, and re-layouts: 25.9 us -> 18.9 us
  other arithmetic: 15 us -> 19.5 us
  starting transfers between devices: 53.2 us -> 48.7 us
    dot_general x12 -> x0, matrix products: 44.6 us -> none  [the longest x8 24.3 us: partial_sum(): lax.dot_general(arrived(step, h), columns, (((0,), (0,)), ((), ())), pref...]
    pallas_call x0 -> x10, Pallas kernels: none -> 37.1 us  [the longest x8 19.5 us: transposed_product(): pl.pallas_call(kernel, out_shape=jax.ShapeDtypeStruct((width, count), jnp...]
    ppermute x39, waiting for transfers between devices: 191 us -> 181 us  [send(): return lax.ppermute(block, AXES, route)]
    dynamic_update_slice x12, local copies, waits for them, and re-layouts: 17.4 us -> 7.97 us  [lined(): result = lax.dynamic_update_slice(result, block, (row, jnp.int32(0)))]
    unnamed x16 -> x42, local copies, waits for them, and re-layouts: 0.84 us -> 8.73 us
    ppermute x39, starting transfers between devices: 53.2 us -> 48.7 us  [send(): return lax.ppermute(block, AXES, route)]
    broadcast_in_dim x1, local copies, waits for them, and re-layouts: 3.94 us -> 0.54 us  [lined(): result = jnp.zeros((n_gx * 2 * block_size, half), jnp.bfloat16)]
  transfers between devices with their start and end apart: 39 -> 39, of which waited for: 17 -> 16; matrix products, arithmetic and copies ran while one was open for 15% -> 9% of each run, Pallas kernels for 0% -> 9%
where the time goes in v1:
time: 307 us; the launch traced here: 306 us
  waiting for transfers between devices  181 us (59%)
  starting transfers between devices  48.7 us (16%)
  Pallas kernels  37.1 us (12%)
  other arithmetic  19.5 us (6%)
  local copies, waits for them, and re-layouts  18.9 us (6%)
    ppermute x39, waiting for transfers between devices, send(): return lax.ppermute(block, AXES, route)  181 us
    ppermute x39, starting transfers between devices, send(): return lax.ppermute(block, AXES, route)  48.7 us
    pallas_call x8, Pallas kernels, transposed_product(): pl.pallas_call(kernel, out_shape=jax.ShapeDtypeStruct((width, count), jnp...  19.5 us
    pallas_call x2, Pallas kernels, advance(): pl.pallas_call(kernel, out_shape=out_shape, in_specs=[smem] + in_vmem(10...  17.6 us
    unnamed x42, local copies, waits for them, and re-layouts  8.73 us
    dynamic_update_slice x12, local copies, waits for them, and re-layouts, lined(): result = lax.dynamic_update_slice(result, block, (row, jnp.int32(0)))  7.97 us
  transfers between devices with their start and end apart: 39, of which 16 were waited for; matrix products, arithmetic and copies ran while one was open for 9% of the time, Pallas kernels for 9%

profile of v1, /device:TPU:0, one launch (start us, length us, event | category | flops | bytes accessed | tf_op | source)
XLA Modules:
  0.0 305.6 jit_solution(17298872085895208622)
XLA Ops:
  0.0 1.7 constant_dynamic-slice_fusion.1
  2.3 1.5 collective-permute-done.15
  3.8 4.9 %collective-permute-start.16 = (bf16[2048,256]{1,0:T(8,128)(2,1)S(1)}, bf16[2048,256]{1,0:T(8,128)(2,1)S(1)}, u32[]{:S(2)}, u32[]{:S(2)}) collective-permute-start(bf16[2048,256]{1,0:T(8,128)(2,1)S(1)} %pad_maximum_fusion.2.refs_0_), channel_id=1, source_target_pairs={{0,2},{1,3},{2,4},{3,5},{4,6},{5,7},{8,10},{9,11},{10,12},{11,13},... | collective-permute-start | bytes 3145736 | tf_op jit(solution)/shard_map/ppermute | solution.py:79
  10.1 1.6 collective-permute-start.6
  11.7 5.6 %collective-permute-start.1 = (bf16[2048,256]{1,0:T(8,128)(2,1)S(1)}, bf16[2048,256]{1,0:T(8,128)(2,1)}, u32[]{:S(2)}, u32[]{:S(2)}) collective-permute-start(bf16[2048,256]{1,0:T(8,128)(2,1)S(1)} %pad_maximum_fusion.1.refs_0_), channel_id=1, source_target_pairs={{0,2},{1,3},{2,4},{3,5},{4,6},{5,7},{8,10},{9,11},{10,12},{11,13},... | collective-permute-start | bytes 3145736 | tf_op jit(solution)/shard_map/ppermute | solution.py:79
  18.6 13.6 %collective-permute-done.16.refs_1_.refs_0_ = bf16[2048,256]{1,0:T(8,128)(2,1)S(1)} collective-permute-done((bf16[2048,256]{1,0:T(8,128)(2,1)S(1)}, bf16[2048,256]{1,0:T(8,128)(2,1)S(1)}, u32[]{:S(2)}, u32[]{:S(2)}) %collective-permute-start.16) | collective-permute-done | bytes 1048608 | tf_op jit(solution)/shard_map/ppermute | solution.py:79
  32.2 1.6 collective-permute-start.17
  33.9 2.9 collective-permute-done.18.refs_2_.refs_1_
  38.1 4.4 %maximum_select_fusion = bf16[1024,1024]{1,0:T(8,128)(2,1)} fusion(bf16[1024,512]{1,0:T(8,128)(2,1)} %collective-permute-done.6, bf16[1024,512]{1,0:T(8,128)(2,1)} %param.5, pred[]{:T(512)S(6)} %eq.34), kind=kLoop, calls=%fused_computation.7 | loop fusion | flops 9437184 | bytes 4194305 | tf_op jit(solution)/shard_map/jit(_where)/select_n | solution.py:295
  42.5 11.4 %collective-permute-done.1.refs_1_.refs_0_ = bf16[2048,256]{1,0:T(8,128)(2,1)} collective-permute-done((bf16[2048,256]{1,0:T(8,128)(2,1)S(1)}, bf16[2048,256]{1,0:T(8,128)(2,1)}, u32[]{:S(2)}, u32[]{:S(2)}) %collective-permute-start.1) | collective-permute-done | bytes 1048608 | tf_op jit(solution)/shard_map/ppermute | solution.py:79
  53.9 1.6 collective-permute-start.2
  55.5 3.8 %collective-permute-done.3.refs_2_.refs_1_ = bf16[2048,256]{1,0:T(8,128)(2,1)} collective-permute-done((bf16[2048,256]{1,0:T(8,128)(2,1)S(1)}, bf16[2048,256]{1,0:T(8,128)(2,1)}, u32[]{:S(2)}, u32[]{:S(2)}) %collective-permute-start.3) | collective-permute-done | bytes 1048608 | tf_op jit(solution)/shard_map/ppermute | solution.py:79
  60.6 21.1 %collective-permute-done.19 = bf16[2048,256]{1,0:T(8,128)(2,1)} collective-permute-done((bf16[2048,256]{1,0:T(8,128)(2,1)}, bf16[2048,256]{1,0:T(8,128)(2,1)}, u32[]{:S(2)}, u32[]{:S(2)}) %collective-permute-start.19) | collective-permute-done | bytes 1048608 | tf_op jit(solution)/shard_map/ppermute | solution.py:79
  81.7 1.3 broadcast_select_fusion.refs_1_.refs_0_
  84.4 19.8 %collective-permute-done.4 = bf16[2048,256]{1,0:T(8,128)(2,1)} collective-permute-done((bf16[2048,256]{1,0:T(8,128)(2,1)}, bf16[2048,256]{1,0:T(8,128)(2,1)}, u32[]{:S(2)}, u32[]{:S(2)}) %collective-permute-start.4) | collective-permute-done | bytes 1048608 | tf_op jit(solution)/shard_map/ppermute | solution.py:79
  104.2 1.3 broadcast_select_fusion.1.refs_1_.refs_0_
  105.6 1.4 collective-permute-start.5
  107.0 2.7 pad_maximum_fusion.refs_2_.refs_3_.refs_1_
  109.7 3.3 %token_product.13 = f32[256,1024]{1,0:T(8,128)S(1)} custom-call(bf16[2048,256]{1,0:T(8,128)(2,1)S(1)} %broadcast_select_fusion.refs_1_.refs_0_, bf16[2048,256]{1,0:T(8,128)(2,1)S(1)} %copy-done.5, bf16[2048,256]{1,0:T(8,128)(2,1)} %collective-permute-done.18.refs_2_.refs_1_, bf16[2048,1024]{1,0:T(8,128)(2,1)S(1)} %pad_maximum_fusion.refs_2_.refs_3_.refs_1_), custom_call_target="tpu_custom_call" | custom-call | flops 1073741824 | bytes 6291456 | tf_op jit(solution)/shard_map/token_product/pallas_call | solution.py:119
  113.0 3.5 %collective-permute-start.24 = (f32[256,1024]{1,0:T(8,128)S(1)}, f32[256,1024]{1,0:T(8,128)S(1)}, u32[]{:S(2)}, u32[]{:S(2)}) collective-permute-start(f32[256,1024]{1,0:T(8,128)S(1)} %token_product.13), channel_id=1, source_target_pairs={{0,16},{1,17},{4,20},{5,21},{8,24},{9,25},{12,28},{13,29},{18,2},{... | collective-permute-start | bytes 3145736 | tf_op jit(solution)/shard_map/ppermute | solution.py:79
  116.5 2.9 token_product.9
  119.4 1.4 collective-permute-start.11
  122.1 3.3 %token_product.10 = f32[256,1024]{1,0:T(8,128)S(1)} custom-call(bf16[2048,256]{1,0:T(8,128)(2,1)} %collective-permute-done.1.refs_1_.refs_0_, bf16[2048,256]{1,0:T(8,128)(2,1)} %collective-permute-done.3.refs_2_.refs_1_, bf16[2048,1024]{1,0:T(8,128)(2,1)S(1)} %pad_maximum_fusion.refs_2_.refs_3_.refs_1_), custom_call_target="tpu_custom_call" | custom-call | flops 1073741824 | bytes 6291456 | tf_op jit(solution)/shard_map/token_product/pallas_call | solution.py:119
  128.0 2.3 token_product.15
  130.2 2.6 token_product.14
  132.8 15.1 %collective-permute-done.5.refs_0_ = bf16[2048,256]{1,0:T(8,128)(2,1)S(1)} collective-permute-done((bf16[2048,256]{1,0:T(8,128)(2,1)S(1)}, bf16[2048,256]{1,0:T(8,128)(2,1)S(1)}, u32[]{:S(2)}, u32[]{:S(2)}) %collective-permute-start.5) | collective-permute-done | bytes 1048608 | tf_op jit(solution)/shard_map/ppermute | solution.py:79
  150.5 2.4 token_product.8.refs_1_
  152.9 6.5 %collective-permute-done.11 = f32[256,1024]{1,0:T(8,128)S(1)} collective-permute-done((f32[256,1024]{1,0:T(8,128)S(1)}, f32[256,1024]{1,0:T(8,128)S(1)}, u32[]{:S(2)}, u32[]{:S(2)}) %collective-permute-start.11) | collective-permute-done | bytes 1048608 | tf_op jit(solution)/shard_map/ppermute | solution.py:79
  159.4 1.6 collective-permute-start.10
  161.0 1.6 collective-permute-start.8
  162.7 13.1 %collective-permute-done.13 = f32[256,1024]{1,0:T(8,128)S(1)} collective-permute-done((f32[256,1024]{1,0:T(8,128)S(1)}, f32[256,1024]{1,0:T(8,128)S(1)}, u32[]{:S(2)}, u32[]{:S(2)}) %collective-permute-start.13) | collective-permute-done | bytes 1048608 | tf_op jit(solution)/shard_map/ppermute | solution.py:79
  176.7 2.3 collective-permute-start.9
  179.0 2.2 copy-done.1
  182.4 1.5 token_product.12.refs_1_
  184.9 1.7 select_select_fusion.2
  186.6 11.7 %collective-permute-done.25 = f32[256,1024]{1,0:T(8,128)} collective-permute-done((f32[256,1024]{1,0:T(8,128)S(1)}, f32[256,1024]{1,0:T(8,128)}, u32[]{:S(2)}, u32[]{:S(2)}) %collective-permute-start.25) | collective-permute-done | bytes 1048608 | tf_op jit(solution)/shard_map/ppermute | solution.py:79
  199.0 18.4 %collective-permute-done.26 = f32[256,1024]{1,0:T(8,128)} collective-permute-done((f32[256,1024]{1,0:T(8,128)}, f32[256,1024]{1,0:T(8,128)}, u32[]{:S(2)}, u32[]{:S(2)}) %collective-permute-start.26) | collective-permute-done | bytes 1048608 | tf_op jit(solution)/shard_map/ppermute | solution.py:79
  217.4 2.6 select_select_fusion
  220.0 1.6 collective-permute-start.22
  222.5 5.4 %fusion = (bf16[1024,1024]{1,0:T(8,128)(2,1)S(1)}, bf16[1024,1024]{1,0:T(8,128)(2,1)S(1)}, bf16[1024,1024]{1,0:T(8,128)(2,1)S(1)}, bf16[1024,1024]{1,0:T(8,128)(2,1)S(1)}) fusion(f32[1,1024,1024]{2,1,0:T(8,128)} %param.6, f32[1,1024,1024]{2,1,0:T(8,128)} %param.7), kind=kLoop, calls=%fused_computation.4 | loop fusion | flops 8388608 | bytes 16777216 | tf_op jit(solution)/shard_map/convert_element_type | solution.py:142
  227.9 9.5 %advance.1 = (f32[1024,1024]{1,0:T(8,128)S(1)}, f32[1]{0:T(128)}) custom-call(f32[1]{0:T(128)} %constant.54.clone.1.refs_0_, f32[256,1024]{1,0:T(8,128)} %token_product.8.refs_1_, f32[256,1024]{1,0:T(8,128)} %collective-permute-done.8.refs_2_, f32[256,1024]{1,0:T(8,128)} %collective-permute-done.9.refs_3_, f32[256,1024]{1,0:T(8,128)} %collective-permute-done.10.refs_4_, ...), custom_call_target="tpu_custom_call" | custom-call | flops 6442450944 | bytes 20971520 | tf_op jit(solution)/shard_map/advance/pallas_call | solution.py:222
  237.4 8.2 %finish.1 = (bf16[1024,512]{1,0:T(8,128)(2,1)S(1)}, bf16[512,512]{1,0:T(8,128)(2,1)S(1)}, bf16[512,512]{1,0:T(8,128)(2,1)S(1)}) custom-call(f32[1]{0:T(128)} %get-tuple-element.16.refs_0_, f32[256,1024]{1,0:T(8,128)S(1)} %token_product.12.refs_1_, f32[256,1024]{1,0:T(8,128)S(1)} %collective-permute-done.21.refs_2_, ...), custom_call_target="tpu_custom_call" | custom-call | flops 6442450944 | bytes 20971520 | tf_op jit(solution)/shard_map/finish/pallas_call | solution.py:222
  246.6 1.5 collective-permute-start.29
  248.6 12.9 %collective-permute-done.29 = bf16[512,512]{1,0:T(8,128)(2,1)} collective-permute-done((bf16[512,512]{1,0:T(8,128)(2,1)S(1)}, bf16[512,512]{1,0:T(8,128)(2,1)}, u32[]{:S(2)}, u32[]{:S(2)}) %collective-permute-start.29) | collective-permute-done | bytes 524320 | tf_op jit(solution)/shard_map/ppermute | solution.py:79
  262.6 9.4 %collective-permute-done.31 = bf16[512,512]{1,0:T(8,128)(2,1)} collective-permute-done((bf16[512,512]{1,0:T(8,128)(2,1)S(1)}, bf16[512,512]{1,0:T(8,128)(2,1)}, u32[]{:S(2)}, u32[]{:S(2)}) %collective-permute-start.31) | collective-permute-done | bytes 524320 | tf_op jit(solution)/shard_map/ppermute | solution.py:79
  273.6 9.5 %collective-permute-done.35 = bf16[512,512]{1,0:T(8,128)(2,1)} collective-permute-done((bf16[512,512]{1,0:T(8,128)(2,1)}, bf16[512,512]{1,0:T(8,128)(2,1)}, u32[]{:S(2)}, u32[]{:S(2)}) %collective-permute-start.35) | collective-permute-done | bytes 524320 | tf_op jit(solution)/shard_map/ppermute | solution.py:79
  283.7 10.1 %collective-permute-done.37 = bf16[512,512]{1,0:T(8,128)(2,1)} collective-permute-done((bf16[512,512]{1,0:T(8,128)(2,1)}, bf16[512,512]{1,0:T(8,128)(2,1)}, u32[]{:S(2)}, u32[]{:S(2)}) %collective-permute-start.37) | collective-permute-done | bytes 524320 | tf_op jit(solution)/shard_map/ppermute | solution.py:79
  301.4 3.4 %copy-done.12 = bf16[8192,512]{1,0:T(8,128)(2,1)} copy-done((bf16[8192,512]{1,0:T(8,128)(2,1)}, bf16[8192,512]{1,0:T(8,128)(2,1)S(1)}, u32[]{:S(2)}) %copy-start.12) | copy-done | bytes 8388632
  (105 shorter events, 31.6 us)
Async XLA Ops:
  1.7 2.1 collective-permute-start.15
  2.2 9.4 %collective-permute-start = (bf16[1024,256]{1,0:T(8,128)(2,1)S(1)}, bf16[1024,256]{1,0:T(8,128)(2,1)S(1)}, u32[]{:S(2)}, u32[]{:S(2)}) collective-permute-start(bf16[1024,256]{1,0:T(8,128)(2,1)S(1)} %get-tuple-element.32), channel_id=1, source_target_pairs={{0,8},{1,9},{2,10},{3,11},{4,12},{5,13},{6,14},{7,15},{8,0},{9,1},... | collective-permute-start | bytes 1572872 | tf_op jit(solution)/shard_map/ppermute | solution.py:79
  3.8 28.4 %collective-permute-start.16 = (bf16[2048,256]{1,0:T(8,128)(2,1)S(1)}, bf16[2048,256]{1,0:T(8,128)(2,1)S(1)}, u32[]{:S(2)}, u32[]{:S(2)}) collective-permute-start(bf16[2048,256]{1,0:T(8,128)(2,1)S(1)} %pad_maximum_fusion.2.refs_0_), channel_id=1, source_target_pairs={{0,2},{1,3},{2,4},{3,5},{4,6},{5,7},{8,10},{9,11},{10,12},{11,13},... | collective-permute-start | bytes 3145736 | tf_op jit(solution)/shard_map/ppermute | solution.py:79
  8.8 28.0 %collective-permute-start.18 = (bf16[2048,256]{1,0:T(8,128)(2,1)S(1)}, bf16[2048,256]{1,0:T(8,128)(2,1)}, u32[]{:S(2)}, u32[]{:S(2)}) collective-permute-start(bf16[2048,256]{1,0:T(8,128)(2,1)S(1)} %pad_maximum_fusion.2.refs_0_), channel_id=1, source_target_pairs={{2,0},{3,1},{4,2},{5,3},{6,4},{7,5},{10,8},{11,9},{12,10},{13,11},... | collective-permute-start | bytes 3145736 | tf_op jit(solution)/shard_map/ppermute | solution.py:79
  10.1 28.0 %collective-permute-start.6 = (bf16[1024,512]{1,0:T(8,128)(2,1)}, bf16[1024,512]{1,0:T(8,128)(2,1)}, u32[]{:S(2)}, u32[]{:S(2)}) collective-permute-start(bf16[1024,512]{1,0:T(8,128)(2,1)} %param.5), channel_id=1, source_target_pairs={{0,1},{1,0},{2,3},{3,2},{4,5},{5,4},{6,7},{7,6},{8,9},{9,8},{10,11... | collective-permute-start | bytes 3145736 | tf_op jit(solution)/shard_map/ppermute | solution.py:79
  11.7 42.1 %collective-permute-start.1 = (bf16[2048,256]{1,0:T(8,128)(2,1)S(1)}, bf16[2048,256]{1,0:T(8,128)(2,1)}, u32[]{:S(2)}, u32[]{:S(2)}) collective-permute-start(bf16[2048,256]{1,0:T(8,128)(2,1)S(1)} %pad_maximum_fusion.1.refs_0_), channel_id=1, source_target_pairs={{0,2},{1,3},{2,4},{3,5},{4,6},{5,7},{8,10},{9,11},{10,12},{11,13},... | collective-permute-start | bytes 3145736 | tf_op jit(solution)/shard_map/ppermute | solution.py:79
  17.3 42.0 %collective-permute-start.3 = (bf16[2048,256]{1,0:T(8,128)(2,1)S(1)}, bf16[2048,256]{1,0:T(8,128)(2,1)}, u32[]{:S(2)}, u32[]{:S(2)}) collective-permute-start(bf16[2048,256]{1,0:T(8,128)(2,1)S(1)} %pad_maximum_fusion.1.refs_0_), channel_id=1, source_target_pairs={{2,0},{3,1},{4,2},{5,3},{6,4},{7,5},{10,8},{11,9},{12,10},{13,11},... | collective-permute-start | bytes 3145736 | tf_op jit(solution)/shard_map/ppermute | solution.py:79
  32.2 28.4 %copy-start.4 = (bf16[2048,256]{1,0:T(8,128)(2,1)}, bf16[2048,256]{1,0:T(8,128)(2,1)S(1)}, u32[]{:S(2)}) copy-start(bf16[2048,256]{1,0:T(8,128)(2,1)S(1)} %collective-permute-done.16.refs_1_.refs_0_) | copy-start | bytes 3145732
  32.2 28.3 %collective-permute-start.17 = (bf16[2048,256]{1,0:T(8,128)(2,1)S(1)}, bf16[2048,256]{1,0:T(8,128)(2,1)}, u32[]{:S(2)}, u32[]{:S(2)}) collective-permute-start(bf16[2048,256]{1,0:T(8,128)(2,1)S(1)} %collective-permute-done.16.refs_1_.refs_0_), channel_id=1, source_target_pairs={{2,4},{3,5},{4,6},{5,7},{10,12},{11,13},{12,14},{13,15},{18,20},{1... | collective-permute-start | bytes 3145736 | tf_op jit(solution)/shard_map/ppermute | solution.py:79
  36.8 44.9 %collective-permute-start.19 = (bf16[2048,256]{1,0:T(8,128)(2,1)}, bf16[2048,256]{1,0:T(8,128)(2,1)}, u32[]{:S(2)}, u32[]{:S(2)}) collective-permute-start(bf16[2048,256]{1,0:T(8,128)(2,1)} %collective-permute-done.18.refs_2_.refs_1_), channel_id=1, source_target_pairs={{2,0},{3,1},{4,2},{5,3},{10,8},{11,9},{12,10},{13,11},{18,16},{19,... | collective-permute-start | bytes 3145736 | tf_op jit(solution)/shard_map/ppermute | solution.py:79
  42.5 64.5 %collective-permute-start.7 = (bf16[1024,1024]{1,0:T(8,128)(2,1)}, bf16[1024,1024]{1,0:T(8,128)(2,1)}, u32[]{:S(2)}, u32[]{:S(2)}) collective-permute-start(bf16[1024,1024]{1,0:T(8,128)(2,1)} %maximum_select_fusion), channel_id=1, source_target_pairs={{0,8},{1,9},{2,10},{3,11},{4,12},{5,13},{6,14},{7,15},{8,0},{9,1},... | collective-permute-start | bytes 6291464 | tf_op jit(solution)/shard_map/ppermute | solution.py:79
  53.9 30.5 %collective-permute-start.2 = (bf16[2048,256]{1,0:T(8,128)(2,1)}, bf16[2048,256]{1,0:T(8,128)(2,1)}, u32[]{:S(2)}, u32[]{:S(2)}) collective-permute-start(bf16[2048,256]{1,0:T(8,128)(2,1)} %collective-permute-done.1.refs_1_.refs_0_), channel_id=1, source_target_pairs={{2,4},{3,5},{4,6},{5,7},{10,12},{11,13},{12,14},{13,15},{18,20},{1... | collective-permute-start | bytes 3145736 | tf_op jit(solution)/shard_map/ppermute | solution.py:79
  59.3 44.9 %collective-permute-start.4 = (bf16[2048,256]{1,0:T(8,128)(2,1)}, bf16[2048,256]{1,0:T(8,128)(2,1)}, u32[]{:S(2)}, u32[]{:S(2)}) collective-permute-start(bf16[2048,256]{1,0:T(8,128)(2,1)} %collective-permute-done.3.refs_2_.refs_1_), channel_id=1, source_target_pairs={{2,0},{3,1},{4,2},{5,3},{10,8},{11,9},{12,10},{13,11},{18,16},{19,... | collective-permute-start | bytes 3145736 | tf_op jit(solution)/shard_map/ppermute | solution.py:79
  83.1 43.6 %collective-permute-start.20 = (bf16[2048,256]{1,0:T(8,128)(2,1)S(1)}, bf16[2048,256]{1,0:T(8,128)(2,1)S(1)}, u32[]{:S(2)}, u32[]{:S(2)}) collective-permute-start(bf16[2048,256]{1,0:T(8,128)(2,1)S(1)} %broadcast_select_fusion.refs_1_.refs_0_), channel_id=1, source_target_pairs={{2,0},{3,1},{4,6},{5,7},{10,8},{11,9},{12,14},{13,15},{18,16},{19,... | collective-permute-start | bytes 3145736 | tf_op jit(solution)/shard_map/ppermute | solution.py:79
  105.6 42.4 %collective-permute-start.5 = (bf16[2048,256]{1,0:T(8,128)(2,1)S(1)}, bf16[2048,256]{1,0:T(8,128)(2,1)S(1)}, u32[]{:S(2)}, u32[]{:S(2)}) collective-permute-start(bf16[2048,256]{1,0:T(8,128)(2,1)S(1)} %broadcast_select_fusion.1.refs_1_.refs_0_), channel_id=1, source_target_pairs={{2,0},{3,1},{4,6},{5,7},{10,8},{11,9},{12,14},{13,15},{18,16},{19,... | collective-permute-start | bytes 3145736 | tf_op jit(solution)/shard_map/ppermute | solution.py:79
  109.7 40.9 %copy-start = (bf16[2048,1024]{1,0:T(8,128)(2,1)}, bf16[2048,1024]{1,0:T(8,128)(2,1)S(1)}, u32[]{:S(2)}) copy-start(bf16[2048,1024]{1,0:T(8,128)(2,1)S(1)} %pad_maximum_fusion.refs_2_.refs_3_.refs_1_) | copy-start | bytes 12582916
  113.0 9.0 %copy-start.6 = (f32[256,1024]{1,0:T(8,128)}, f32[256,1024]{1,0:T(8,128)S(1)}, u32[]{:S(2)}) copy-start(f32[256,1024]{1,0:T(8,128)S(1)} %token_product.13) | copy-start | bytes 3145732
  113.0 36.2 %collective-permute-start.24 = (f32[256,1024]{1,0:T(8,128)S(1)}, f32[256,1024]{1,0:T(8,128)S(1)}, u32[]{:S(2)}, u32[]{:S(2)}) collective-permute-start(f32[256,1024]{1,0:T(8,128)S(1)} %token_product.13), channel_id=1, source_target_pairs={{0,16},{1,17},{4,20},{5,21},{8,24},{9,25},{12,28},{13,29},{18,2},{... | collective-permute-start | bytes 3145736 | tf_op jit(solution)/shard_map/ppermute | solution.py:79
  119.4 40.0 %collective-permute-start.11 = (f32[256,1024]{1,0:T(8,128)S(1)}, f32[256,1024]{1,0:T(8,128)S(1)}, u32[]{:S(2)}, u32[]{:S(2)}) collective-permute-start(f32[256,1024]{1,0:T(8,128)S(1)} %token_product.9), channel_id=1, source_target_pairs={{0,16},{1,17},{4,20},{5,21},{8,24},{9,25},{12,28},{13,29},{18,2},{... | collective-permute-start | bytes 3145736 | tf_op jit(solution)/shard_map/ppermute | solution.py:79
  122.1 8.2 %copy-start.2 = (f32[256,1024]{1,0:T(8,128)}, f32[256,1024]{1,0:T(8,128)S(1)}, u32[]{:S(2)}) copy-start(f32[256,1024]{1,0:T(8,128)S(1)} %token_product.11) | copy-start | bytes 3145732
  125.3 35.7 %collective-permute-start.12 = (f32[256,1024]{1,0:T(8,128)S(1)}, f32[256,1024]{1,0:T(8,128)S(1)}, u32[]{:S(2)}, u32[]{:S(2)}) collective-permute-start(f32[256,1024]{1,0:T(8,128)S(1)} %token_product.10), channel_id=1, source_target_pairs={{2,18},{3,19},{6,22},{7,23},{10,26},{11,27},{14,30},{15,31},{16,0}... | collective-permute-start | bytes 3145736 | tf_op jit(solution)/shard_map/ppermute | solution.py:79
  126.7 49.1 %collective-permute-start.13 = (f32[256,1024]{1,0:T(8,128)S(1)}, f32[256,1024]{1,0:T(8,128)S(1)}, u32[]{:S(2)}, u32[]{:S(2)}) collective-permute-start(f32[256,1024]{1,0:T(8,128)S(1)} %token_product.11), channel_id=1, source_target_pairs={{4,20},{5,21},{6,22},{7,23},{12,28},{13,29},{14,30},{15,31},{16,0}... | collective-permute-start | bytes 3145736 | tf_op jit(solution)/shard_map/ppermute | solution.py:79
  147.9 50.4 %collective-permute-start.25 = (f32[256,1024]{1,0:T(8,128)S(1)}, f32[256,1024]{1,0:T(8,128)}, u32[]{:S(2)}, u32[]{:S(2)}) collective-permute-start(f32[256,1024]{1,0:T(8,128)S(1)} %token_product.14), channel_id=1, source_target_pairs={{2,18},{3,19},{6,22},{7,23},{10,26},{11,27},{14,30},{15,31},{16,0}... | collective-permute-start | bytes 3145736 | tf_op jit(solution)/shard_map/ppermute | solution.py:79
  149.2 26.5 %copy-start.13 = (f32[256,1024]{1,0:T(8,128)}, f32[256,1024]{1,0:T(8,128)S(1)}, u32[]{:S(2)}) copy-start(f32[256,1024]{1,0:T(8,128)S(1)} %collective-permute-done.24) | copy-start | bytes 3145732
  149.2 68.2 %collective-permute-start.26 = (f32[256,1024]{1,0:T(8,128)}, f32[256,1024]{1,0:T(8,128)}, u32[]{:S(2)}, u32[]{:S(2)}) collective-permute-start(f32[256,1024]{1,0:T(8,128)} %token_product.15), channel_id=1, source_target_pairs={{4,20},{5,21},{6,22},{7,23},{12,28},{13,29},{14,30},{15,31},{16,0}... | collective-permute-start | bytes 3145736 | tf_op jit(solution)/shard_map/ppermute | solution.py:79
  159.4 16.4 %copy-start.15 = (f32[256,1024]{1,0:T(8,128)}, f32[256,1024]{1,0:T(8,128)S(1)}, u32[]{:S(2)}) copy-start(f32[256,1024]{1,0:T(8,128)S(1)} %collective-permute-done.11) | copy-start | bytes 3145732
  159.4 60.6 %collective-permute-start.10 = (f32[256,1024]{1,0:T(8,128)}, f32[256,1024]{1,0:T(8,128)}, u32[]{:S(2)}, u32[]{:S(2)}) collective-permute-start(f32[256,1024]{1,0:T(8,128)} %token_product.8.refs_1_), channel_id=1, source_target_pairs={{12,4},{13,5},{14,6},{15,7},{16,24},{17,25},{18,26},{19,27}} | collective-permute-start | bytes 3145736 | tf_op jit(solution)/shard_map/ppermute | solution.py:79
  161.0 14.7 %copy-start.17 = (f32[256,1024]{1,0:T(8,128)}, f32[256,1024]{1,0:T(8,128)S(1)}, u32[]{:S(2)}) copy-start(f32[256,1024]{1,0:T(8,128)S(1)} %collective-permute-done.12) | copy-start | bytes 3145732
  161.0 60.6 %collective-permute-start.8 = (f32[256,1024]{1,0:T(8,128)}, f32[256,1024]{1,0:T(8,128)}, u32[]{:S(2)}, u32[]{:S(2)}) collective-permute-start(f32[256,1024]{1,0:T(8,128)} %token_product.8.refs_1_), channel_id=1, source_target_pairs={{8,24},{9,25},{10,26},{11,27},{20,4},{21,5},{22,6},{23,7}} | collective-permute-start | bytes 3145736 | tf_op jit(solution)/shard_map/ppermute | solution.py:79
  176.7 45.7 %collective-permute-start.9 = (f32[256,1024]{1,0:T(8,128)}, f32[256,1024]{1,0:T(8,128)}, u32[]{:S(2)}, u32[]{:S(2)}) collective-permute-start(f32[256,1024]{1,0:T(8,128)} %token_product.8.refs_1_), channel_id=1, source_target_pairs={{0,24},{1,25},{2,26},{3,27},{28,4},{29,5},{30,6},{31,7}} | collective-permute-start | bytes 3145736 | tf_op jit(solution)/shard_map/ppermute | solution.py:79
  184.9 32.5 %copy-start.7 = (f32[256,1024]{1,0:T(8,128)S(1)}, f32[256,1024]{1,0:T(8,128)}, u32[]{:S(2)}) copy-start(f32[256,1024]{1,0:T(8,128)} %copy-done.6) | copy-start | bytes 3145732
  184.9 32.5 %copy-start.14 = (f32[256,1024]{1,0:T(8,128)S(1)}, f32[256,1024]{1,0:T(8,128)}, u32[]{:S(2)}) copy-start(f32[256,1024]{1,0:T(8,128)} %copy-done.13) | copy-start | bytes 3145732
  198.3 39.1 %collective-permute-start.21 = (f32[256,1024]{1,0:T(8,128)S(1)}, f32[256,1024]{1,0:T(8,128)S(1)}, u32[]{:S(2)}, u32[]{:S(2)}) collective-permute-start(f32[256,1024]{1,0:T(8,128)S(1)} %token_product.12.refs_1_), channel_id=1, source_target_pairs={{8,24},{9,25},{10,26},{11,27},{20,4},{21,5},{22,6},{23,7}} | collective-permute-start | bytes 3145736 | tf_op jit(solution)/shard_map/ppermute | solution.py:79
  217.4 10.4 %collective-permute-start.14 = (f32[256,1024]{1,0:T(8,128)}, f32[256,1024]{1,0:T(8,128)S(1)}, u32[]{:S(2)}, u32[]{:S(2)}) collective-permute-start(f32[256,1024]{1,0:T(8,128)} %get-tuple-element.15), channel_id=1, source_target_pairs={{0,8},{1,9},{2,10},{3,11},{4,12},{5,13},{6,14},{7,15},{8,0},{9,1},... | collective-permute-start | bytes 3145736 | tf_op jit(solution)/shard_map/ppermute | solution.py:79
  220.0 17.3 %collective-permute-start.22 = (f32[256,1024]{1,0:T(8,128)S(1)}, f32[256,1024]{1,0:T(8,128)S(1)}, u32[]{:S(2)}, u32[]{:S(2)}) collective-permute-start(f32[256,1024]{1,0:T(8,128)S(1)} %token_product.12.refs_1_), channel_id=1, source_target_pairs={{0,24},{1,25},{2,26},{3,27},{28,4},{29,5},{30,6},{31,7}} | collective-permute-start | bytes 3145736 | tf_op jit(solution)/shard_map/ppermute | solution.py:79
  221.7 15.7 %collective-permute-start.23 = (f32[256,1024]{1,0:T(8,128)S(1)}, f32[256,1024]{1,0:T(8,128)S(1)}, u32[]{:S(2)}, u32[]{:S(2)}) collective-permute-start(f32[256,1024]{1,0:T(8,128)S(1)} %token_product.12.refs_1_), channel_id=1, source_target_pairs={{12,4},{13,5},{14,6},{15,7},{16,24},{17,25},{18,26},{19,27}} | collective-permute-start | bytes 3145736 | tf_op jit(solution)/shard_map/ppermute | solution.py:79
  222.4 15.0 %collective-permute-start.27 = (f32[256,1024]{1,0:T(8,128)S(1)}, f32[256,1024]{1,0:T(8,128)S(1)}, u32[]{:S(2)}, u32[]{:S(2)}) collective-permute-start(f32[256,1024]{1,0:T(8,128)S(1)} %get-tuple-element.18), channel_id=1, source_target_pairs={{0,8},{1,9},{2,10},{3,11},{4,12},{5,13},{6,14},{7,15},{8,0},{9,1},... | collective-permute-start | bytes 3145736 | tf_op jit(solution)/shard_map/ppermute | solution.py:79
  245.6 27.5 %collective-permute-start.33 = (bf16[1024,512]{1,0:T(8,128)(2,1)S(1)}, bf16[1024,512]{1,0:T(8,128)(2,1)S(1)}, u32[]{:S(2)}, u32[]{:S(2)}) collective-permute-start(bf16[1024,512]{1,0:T(8,128)(2,1)S(1)} %get-tuple-element.20), channel_id=1, source_target_pairs={{0,16},{1,17},{2,18},{3,19},{4,20},{5,21},{6,22},{7,23},{8,24},{9,... | collective-permute-start | bytes 3145736 | tf_op jit(solution)/shard_map/ppermute | solution.py:79
  246.6 14.9 %collective-permute-start.29 = (bf16[512,512]{1,0:T(8,128)(2,1)S(1)}, bf16[512,512]{1,0:T(8,128)(2,1)}, u32[]{:S(2)}, u32[]{:S(2)}) collective-permute-start(bf16[512,512]{1,0:T(8,128)(2,1)S(1)} %get-tuple-element.21), channel_id=1, source_target_pairs={{0,1},{1,0},{2,3},{3,2},{4,5},{5,4},{6,7},{7,6},{8,9},{9,8},{10,11... | collective-permute-start | bytes 1572872 | tf_op jit(solution)/shard_map/ppermute | solution.py:79
  248.1 23.9 %collective-permute-start.31 = (bf16[512,512]{1,0:T(8,128)(2,1)S(1)}, bf16[512,512]{1,0:T(8,128)(2,1)}, u32[]{:S(2)}, u32[]{:S(2)}) collective-permute-start(bf16[512,512]{1,0:T(8,128)(2,1)S(1)} %get-tuple-element.22), channel_id=1, source_target_pairs={{0,1},{1,0},{2,3},{3,2},{4,5},{5,4},{6,7},{7,6},{8,9},{9,8},{10,11... | collective-permute-start | bytes 1572872 | tf_op jit(solution)/shard_map/ppermute | solution.py:79
  248.6 45.1 %collective-permute-start.28 = (bf16[1024,512]{1,0:T(8,128)(2,1)S(1)}, bf16[1024,512]{1,0:T(8,128)(2,1)}, u32[]{:S(2)}, u32[]{:S(2)}) collective-permute-start(bf16[1024,512]{1,0:T(8,128)(2,1)S(1)} %get-tuple-element.20), channel_id=1, source_target_pairs={{0,8},{1,9},{2,10},{3,11},{4,12},{5,13},{6,14},{7,15},{8,0},{9,1},... | collective-permute-start | bytes 3145736 | tf_op jit(solution)/shard_map/ppermute | solution.py:79
  261.5 21.5 %collective-permute-start.35 = (bf16[512,512]{1,0:T(8,128)(2,1)}, bf16[512,512]{1,0:T(8,128)(2,1)}, u32[]{:S(2)}, u32[]{:S(2)}) collective-permute-start(bf16[512,512]{1,0:T(8,128)(2,1)} %collective-permute-done.29), channel_id=1, source_target_pairs={{0,16},{1,17},{2,18},{3,19},{4,20},{5,21},{6,22},{7,23},{8,24},{9,... | collective-permute-start | bytes 1572872 | tf_op jit(solution)/shard_map/ppermute | solution.py:79
  272.0 21.8 %collective-permute-start.37 = (bf16[512,512]{1,0:T(8,128)(2,1)}, bf16[512,512]{1,0:T(8,128)(2,1)}, u32[]{:S(2)}, u32[]{:S(2)}) collective-permute-start(bf16[512,512]{1,0:T(8,128)(2,1)} %collective-permute-done.31), channel_id=1, source_target_pairs={{0,16},{1,17},{2,18},{3,19},{4,20},{5,21},{6,22},{7,23},{8,24},{9,... | collective-permute-start | bytes 1572872 | tf_op jit(solution)/shard_map/ppermute | solution.py:79
  273.0 26.0 %collective-permute-start.34 = (bf16[1024,512]{1,0:T(8,128)(2,1)S(1)}, bf16[1024,512]{1,0:T(8,128)(2,1)S(1)}, u32[]{:S(2)}, u32[]{:S(2)}) collective-permute-start(bf16[1024,512]{1,0:T(8,128)(2,1)S(1)} %collective-permute-done.33), channel_id=1, source_target_pairs={{0,8},{1,9},{2,10},{3,11},{4,12},{5,13},{6,14},{7,15},{8,0},{9,1},... | collective-permute-start | bytes 3145736 | tf_op jit(solution)/shard_map/ppermute | solution.py:79
  273.0 23.6 %collective-permute-start.30 = (bf16[512,512]{1,0:T(8,128)(2,1)}, bf16[512,512]{1,0:T(8,128)(2,1)}, u32[]{:S(2)}, u32[]{:S(2)}) collective-permute-start(bf16[512,512]{1,0:T(8,128)(2,1)} %collective-permute-done.29), channel_id=1, source_target_pairs={{0,8},{1,9},{2,10},{3,11},{4,12},{5,13},{6,14},{7,15},{8,0},{9,1},... | collective-permute-start | bytes 1572872 | tf_op jit(solution)/shard_map/ppermute | solution.py:79
  283.0 15.9 %collective-permute-start.32 = (bf16[512,512]{1,0:T(8,128)(2,1)}, bf16[512,512]{1,0:T(8,128)(2,1)S(1)}, u32[]{:S(2)}, u32[]{:S(2)}) collective-permute-start(bf16[512,512]{1,0:T(8,128)(2,1)} %collective-permute-done.31), channel_id=1, source_target_pairs={{0,8},{1,9},{2,10},{3,11},{4,12},{5,13},{6,14},{7,15},{8,0},{9,1},... | collective-permute-start | bytes 1572872 | tf_op jit(solution)/shard_map/ppermute | solution.py:79
  293.8 6.5 %collective-permute-start.36 = (bf16[512,512]{1,0:T(8,128)(2,1)}, bf16[512,512]{1,0:T(8,128)(2,1)S(1)}, u32[]{:S(2)}, u32[]{:S(2)}) collective-permute-start(bf16[512,512]{1,0:T(8,128)(2,1)} %collective-permute-done.35), channel_id=1, source_target_pairs={{0,8},{1,9},{2,10},{3,11},{4,12},{5,13},{6,14},{7,15},{8,0},{9,1},... | collective-permute-start | bytes 1572872 | tf_op jit(solution)/shard_map/ppermute | solution.py:79
  293.8 7.6 %collective-permute-start.38 = (bf16[512,512]{1,0:T(8,128)(2,1)}, bf16[512,512]{1,0:T(8,128)(2,1)S(1)}, u32[]{:S(2)}, u32[]{:S(2)}) collective-permute-start(bf16[512,512]{1,0:T(8,128)(2,1)} %collective-permute-done.37), channel_id=1, source_target_pairs={{0,8},{1,9},{2,10},{3,11},{4,12},{5,13},{6,14},{7,15},{8,0},{9,1},... | collective-permute-start | bytes 1572872 | tf_op jit(solution)/shard_map/ppermute | solution.py:79
  (12 other events, 33.7 us)

commit v2 on v1

--- a/solution.py
+++ b/solution.py
@@ -92,7 +92,7 @@
     return gx // 2, gx % 2, gy // 2, gy % 2
 
 
-def transposed_product(choices, columns, pick):
+def transposed_product(choices, columns, pick, strips):
     contracted, width = choices[0].shape
     count = columns.shape[1]
 
@@ -109,12 +109,19 @@
             for number, choice_ref in enumerate(choice_refs):
                 pl.when(index == number)(lambda ref=choice_ref: take(ref))
 
-        out_ref[...] = lax.dot_general(
-            taken_ref[...],
-            columns_ref[...],
-            (((0,), (0,)), ((), ())),
-            preferred_element_type=jnp.float32,
-        )
+        strip = count // strips
+
+        def step(number, carry):
+            at = pl.ds(pl.multiple_of(number * strip, strip), strip)
+            out_ref[:, at] = lax.dot_general(
+                taken_ref[...],
+                columns_ref[:, at],
+                (((0,), (0,)), ((), ())),
+                preferred_element_type=jnp.float32,
+            )
+            return carry
+
+        lax.fori_loop(0, strips, step, 0, unroll=strips == 1)
 
     return pl.pallas_call(
         kernel,
@@ -149,29 +156,46 @@
     return single(left[0], right[0]) + (single(left[0], right[1]) + single(left[1], right[0]))
 
 
-def advance(squares, sums, left, right, so_far, final, low, last):
+def advance(squares, sums, left, right, so_far, final, low, outputs):
     width = sums[0].shape[0]
     size = right[0].shape[0]
     half = size // 2
     strip = size // STRIPS
     given = 0 if so_far is None else 1
-
-    def kernel(*refs):
-        squares_ref, part, same, cross, mate, mine, theirs, lh, ll, rh, rl = refs[:11]
-        acc = refs[11] if given else None
-        outs, (shaped, rows) = refs[11 + given : -2], refs[-2:]
-        if not last:
+    late = len(sums) > 2
+    unrolled = outputs > 0 or late
+
+    def kernel(squares_ref, *refs):
+        sum_refs, refs = refs[: len(sums)], refs[len(sums) :]
+        (lh, ll, rh, rl), refs = refs[:4], refs[4:]
+        acc, refs = (refs[0], refs[1:]) if given else (None, refs)
+        outs, (shaped, rows, inner_high, inner_low) = refs[:-4], refs[-4:]
+        if not outputs:
             shaped = outs[0]
         x, core, z, y = whereabouts()
-        is_last = chosen(final, z) == 2 * x + core
-        my_rows = jnp.where(is_last, part[...] + same[...], mine[...])
-        their_rows = jnp.where(is_last, cross[...] + mate[...], theirs[...])
+        my_rows, their_rows = sum_refs[0][...], sum_refs[1][...]
+        if late:
+            part, same, cross, mate = sum_refs[2:]
+            is_last = chosen(final, z) == 2 * x + core
+            my_rows = jnp.where(is_last, part[...] + same[...], my_rows)
+            their_rows = jnp.where(is_last, cross[...] + mate[...], their_rows)
         rows[:width] = jnp.where(core == 0, my_rows, their_rows)
         rows[width:] = jnp.where(core == 0, their_rows, my_rows)
         entry = squares_ref[0] + jnp.sum(my_rows * my_rows) + jnp.sum(their_rows * their_rows)
         piece = halves(rows[...])
-
-        inner = halves(three_pass(piece, (rh[...], rl[...])))
+        if unrolled:
+            inner_high[...], inner_low[...] = halves(three_pass(piece, (rh[...], rl[...])))
+        else:
+
+            def first(number, carry):
+                at = pl.ds(pl.multiple_of(number * strip, strip), strip)
+                high, low = halves(three_pass(piece, (rh[:, at], rl[:, at])))
+                inner_high[:, at] = high
+                inner_low[:, at] = low
+                return carry
+
+            lax.fori_loop(0, STRIPS, first, 0)
+        inner = inner_high[...], inner_low[...]
 
         def second(number, total):
             at = pl.ds(pl.multiple_of(number * strip, strip), strip)
@@ -185,56 +209,92 @@
             if given:
                 block = acc[at] + block
             shaped[at] = block
-            return total + jnp.sum(block * block) if last else total
-
-        result = lax.fori_loop(0, STRIPS, second, jnp.float32(0), unroll=True)
-        if not last:
+            return total + jnp.sum(block * block) if outputs else total
+
+        result = lax.fori_loop(0, STRIPS, second, jnp.float32(0), unroll=unrolled)
+        if not outputs:
             outs[1][0] = entry
             return
-        near, far_0, far_1 = outs
         count = size * size
         graft = jnp.sqrt(entry / count + epsilon) / jnp.sqrt(result / count + epsilon)
 
         def store(near_columns, far_columns):
-            near[...] = (shaped[:, near_columns] * graft).astype(jnp.bfloat16)
-            far_0[...] = (shaped[:half, far_columns] * graft).astype(jnp.bfloat16)
-            far_1[...] = (shaped[half:, far_columns] * graft).astype(jnp.bfloat16)
+            outs[0][...] = (shaped[:, near_columns] * graft).astype(jnp.bfloat16)
+            if outputs == 3:
+                outs[1][...] = (shaped[:half, far_columns] * graft).astype(jnp.bfloat16)
+                outs[2][...] = (shaped[half:, far_columns] * graft).astype(jnp.bfloat16)
 
         one, other = pl.ds(0, half), pl.ds(half, half)
         pl.when(y == 0)(lambda: store(one, other))
         pl.when(y == 1)(lambda: store(other, one))
 
     smem = pl.BlockSpec(memory_space=pltpu.SMEM)
-    if last:
-        out_shape = [
-            jax.ShapeDtypeStruct((size, half), jnp.bfloat16),
-            jax.ShapeDtypeStruct((half, half), jnp.bfloat16),
-            jax.ShapeDtypeStruct((half, half), jnp.bfloat16),
-        ]
-        out_specs = in_vmem(3)
+    if outputs:
+        shapes = [(size, half), (half, half), (half, half)][:outputs]
+        out_shape = [jax.ShapeDtypeStruct(shape, jnp.bfloat16) for shape in shapes]
+        out_specs = in_vmem(outputs)
     else:
         out_shape = [
             jax.ShapeDtypeStruct((size, size), jnp.float32),
             jax.ShapeDtypeStruct((1,), jnp.float32),
         ]
         out_specs = in_vmem(1) + [smem]
-    scratch_size = size if last else 8
     return pl.pallas_call(
         kernel,
         out_shape=out_shape,
-        in_specs=[smem] + in_vmem(10 + given),
+        in_specs=[smem] + in_vmem(len(sums) + 4 + given),
         out_specs=out_specs,
-        input_output_aliases={11: 0} if given and not last else {},
         scratch_shapes=[
-            pltpu.VMEM((scratch_size, size), jnp.float32),
+            pltpu.VMEM((size if outputs else 8, size), jnp.float32),
             pltpu.VMEM((2 * width, size), jnp.float32),
+            pltpu.VMEM((2 * width, size), jnp.bfloat16),
+            pltpu.VMEM((2 * width, size), jnp.bfloat16),
         ],
         cost_estimate=pl.CostEstimate(
             flops=24 * width * size * size, transcendentals=0, bytes_accessed=20 * size * size
         ),
-        compiler_params=params(24 if last else 16),
-        name="finish" if last else "advance",
+        compiler_params=params(24 if outputs else 16),
+        name="finish" if outputs else "advance",
     )(squares, *sums, *left, *right, *([so_far] if given else []))
+
+
+def put(result, blocks, places, height, block_size):
+    width = blocks[0].shape[1]
+    given = 0 if result is None else 1
+
+    def kernel(*refs):
+        block_refs, out_ref, sems = refs[: len(blocks)], refs[-2], refs[-1]
+        x, core, _, y = whereabouts()
+        copies = []
+        for number, (ref, (dx, dc, dy, offset)) in enumerate(zip(block_refs, places)):
+            from_x = 1 - x if dx else x
+            from_core = 1 - core if dc else core
+            from_y = 1 - y if dy else y
+            row = (4 * from_x + 2 * from_core + from_y) * block_size + offset
+            row = pl.multiple_of(row, block_size // 2)
+            target = out_ref.at[pl.ds(row, ref.shape[0])]
+            copies.append(pltpu.make_async_copy(ref, target, sems.at[number]))
+        for copy in copies:
+            copy.start()
+        for copy in copies:
+            copy.wait()
+
+    anywhere = pl.BlockSpec(memory_space=pl.ANY)
+    return pl.pallas_call(
+        kernel,
+        out_shape=jax.ShapeDtypeStruct((height, width), blocks[0].dtype),
+        in_specs=in_vmem(len(blocks)) + [anywhere] * given,
+        out_specs=anywhere,
+        scratch_shapes=[pltpu.SemaphoreType.DMA((len(blocks),))],
+        input_output_aliases={len(blocks): 0} if given else {},
+        cost_estimate=pl.CostEstimate(
+            flops=2 * sum(block.size for block in blocks) * 256,
+            transcendentals=0,
+            bytes_accessed=4 * sum(block.size for block in blocks),
+        ),
+        compiler_params=params(16),
+        name="put",
+    )(*blocks, *([result] if given else []))
 
 
 def chosen(table, z):
@@ -307,19 +367,23 @@
             return (z == 0) | (z == n_z - 1)
 
         if step == 0:
-            return transposed_product([own[h]], columns, None)
+            return transposed_product([own[h]], columns, None, STRIPS)
         if step == 1:
             return transposed_product(
-                [first_up[h], first_down[h]], columns, lambda z: jnp.where(lower(z), 1, 0)
+                [first_up[h], first_down[h]],
+                columns,
+                lambda z: jnp.where(lower(z), 1, 0),
+                STRIPS,
             )
         if step == 2:
             return transposed_product(
                 [second[h], first_up[h], first_down[h]],
                 columns,
                 lambda z: jnp.where(at_end(z), 0, jnp.where(lower(z), 1, 2)),
+                STRIPS,
             )
         return transposed_product(
-            [third[h], second[h]], columns, lambda z: jnp.where(at_end(z), 0, 1)
+            [third[h], second[h]], columns, lambda z: jnp.where(at_end(z), 0, 1), 1
         )
 
     tables = [[0, 1, 2, 3], [1, 2, 1, 2], [2, 0, 3, 1], [3, 3, 0, 0]]
@@ -341,7 +405,8 @@
         else None
     )
     shaped = None
-    squares = jnp.zeros((1,), jnp.float32)
+    squares = early_squares = jnp.zeros((1,), jnp.float32)
+    early_shaped = None
     left, right = kept_halves(left_root), kept_halves(right_root)
     for h in pieces:
         mine = theirs = None
@@ -362,43 +427,62 @@
                 theirs = jnp.where(sources[step] == 2 * x + 1 - core, total, theirs)
         mine, theirs = lax.optimization_barrier((mine, theirs))
         theirs = moved(theirs, across_cores)
+        final_piece = h == len(widths) - 1
+        early = advance(
+            early_squares,
+            (mine, theirs),
+            left,
+            right,
+            early_shaped,
+            final,
+            starts[h],
+            1 if final_piece else 0,
+        )
+        if not final_piece:
+            early_shaped, early_squares = early
         part = partial_sum(3, h)
         from_same = moved(part, same_core)
         from_cross = moved(part, cross_core)
         from_mate = moved(part, chip_mate)
-        final_piece = h == len(widths) - 1
         outcome = advance(
             squares,
-            (part, from_same, from_cross, from_mate, mine, theirs),
+            (mine, theirs, part, from_same, from_cross, from_mate),
             left,
             right,
             shaped,
             final,
             starts[h],
-            final_piece,
+            3 if final_piece else 0,
         )
         if not final_piece:
             shaped, squares = outcome
     near, *far_parts = outcome
 
-    across = moved(near, across_x)
+    early_route = route(lambda x, c, z, y: (1 - x, c, z, y) if 2 * x + c != final[z] else None)
+    late_route = route(lambda x, c, z, y: (1 - x, c, z, y) if 2 * x + c == final[z] else None)
+    across = jnp.where(
+        sources[3] == 2 * (1 - x) + core, moved(near, late_route), moved(early[0], early_route)
+    )
     beside = [moved(part, across_y) for part in far_parts]
     diagonal = [moved(part, across_x) for part in beside]
     depth = block_size // 2
     parts = [
-        (near, x, y, 0),
-        (beside[0], x, 1 - y, 0),
-        (beside[1], x, 1 - y, depth),
-        (across, 1 - x, y, 0),
-        (diagonal[0], 1 - x, 1 - y, 0),
-        (diagonal[1], 1 - x, 1 - y, depth),
+        (near, 0, 0, 0),
+        (beside[0], 0, 1, 0),
+        (beside[1], 0, 1, depth),
+        (across, 1, 0, 0),
+        (diagonal[0], 1, 1, 0),
+        (diagonal[1], 1, 1, depth),
     ]
-    result = jnp.zeros((n_gx * 2 * block_size, half), jnp.bfloat16)
-    for part, from_x, from_y, offset in parts:
-        other = moved(part, across_cores)
-        for block, from_core in ((part, core), (other, 1 - core)):
-            row = (4 * from_x + 2 * from_core + from_y) * block_size + offset
-            result = lax.dynamic_update_slice(result, block, (row, jnp.int32(0)))
+    others = [moved(part, across_cores) for part, *_ in parts]
+    result = None
+    for members in ((0, 1, 2, 3), (4,), (5,)):
+        blocks, places = [], []
+        for member in members:
+            part, dx, dy, offset = parts[member]
+            blocks += [part, others[member]]
+            places += [(dx, 0, dy, offset), (dx, 1, dy, offset)]
+        result = put(result, blocks, places, n_gx * 2 * block_size, block_size)
     return result
 
 

time: 307 us -> 317 us (1.033)
  waiting for transfers between devices: 181 us -> 150 us
  Pallas kernels: 37.1 us -> 62.7 us
  starting transfers between devices: 48.7 us -> 74.3 us
  local copies, waits for them, and re-layouts: 18.9 us -> 7.22 us
    ppermute x39 -> x40, waiting for transfers between devices: 181 us -> 150 us  [send(): return lax.ppermute(block, AXES, route)]
    ppermute x39 -> x40, starting transfers between devices: 48.7 us -> 74.3 us  [send(): return lax.ppermute(block, AXES, route)]
    pallas_call x2 -> x7, Pallas kernels: 17.6 us -> 40.2 us  [the longest x4 35.5 us: advance(): pl.pallas_call(kernel, out_shape=out_shape, in_specs=[smem] + in_vmem(len...]
    dynamic_update_slice x12 -> x0, local copies, waits for them, and re-layouts: 7.97 us -> none  [lined(): result = lax.dynamic_update_slice(result, block, (row, jnp.int32(0)))]
    unnamed x42 -> x40, local copies, waits for them, and re-layouts: 8.73 us -> 5.54 us
  transfers between devices with their start and end apart: 39 -> 40, of which waited for: 16 -> 17; matrix products, arithmetic and copies ran while one was open for 9% -> 7% of each run, Pallas kernels for 9% -> 17%
where the time goes in v2:
time: 317 us; the launch traced here: 315 us
  waiting for transfers between devices  150 us (47%)
  starting transfers between devices  74.3 us (23%)
  Pallas kernels  62.7 us (20%)
  other arithmetic  20.8 us (7%)
  local copies, waits for them, and re-layouts  7.22 us (2%)
    ppermute x40, waiting for transfers between devices, send(): return lax.ppermute(block, AXES, route)  150 us
    ppermute x40, starting transfers between devices, send(): return lax.ppermute(block, AXES, route)  74.3 us
    pallas_call x4, Pallas kernels, advance(): pl.pallas_call(kernel, out_shape=out_shape, in_specs=[smem] + in_vmem(len...  35.5 us
    pallas_call x8, Pallas kernels, transposed_product(): pl.pallas_call(kernel, out_shape=jax.ShapeDtypeStruct((width, count), jnp...  22.5 us
  transfers between devices with their start and end apart: 40, of which 17 were waited for; matrix products, arithmetic and copies ran while one was open for 7% of the time, Pallas kernels for 17%

profile of v2, /device:TPU:0, one launch (start us, length us, event | category | flops | bytes accessed | tf_op | source)
XLA Modules:
  0.0 315.5 jit_solution(1789332759813711196)
XLA Ops:
  0.0 1.7 constant_dynamic-slice_fusion.1
  5.1 6.4 %collective-permute-start.16 = (bf16[2048,256]{1,0:T(8,128)(2,1)S(1)}, bf16[2048,256]{1,0:T(8,128)(2,1)}, u32[]{:S(2)}, u32[]{:S(2)}) collective-permute-start(bf16[2048,256]{1,0:T(8,128)(2,1)S(1)} %pad_maximum_fusion.2.refs_0_), channel_id=1, source_target_pairs={{0,2},{1,3},{2,4},{3,5},{4,6},{5,7},{8,10},{9,11},{10,12},{11,13},... | collective-permute-start | bytes 3145736 | tf_op jit(solution)/shard_map/ppermute | solution.py:79
  11.6 2.0 collective-permute-start.5
  14.9 5.6 %collective-permute-start.1 = (bf16[2048,256]{1,0:T(8,128)(2,1)S(1)}, bf16[2048,256]{1,0:T(8,128)(2,1)}, u32[]{:S(2)}, u32[]{:S(2)}) collective-permute-start(bf16[2048,256]{1,0:T(8,128)(2,1)S(1)} %pad_maximum_fusion.1.refs_0_), channel_id=1, source_target_pairs={{0,2},{1,3},{2,4},{3,5},{4,6},{5,7},{8,10},{9,11},{10,12},{11,13},... | collective-permute-start | bytes 3145736 | tf_op jit(solution)/shard_map/ppermute | solution.py:79
  20.5 12.2 %collective-permute-done.18.refs_2_.refs_1_ = bf16[2048,256]{1,0:T(8,128)(2,1)S(1)} collective-permute-done((bf16[2048,256]{1,0:T(8,128)(2,1)S(1)}, bf16[2048,256]{1,0:T(8,128)(2,1)S(1)}, u32[]{:S(2)}, u32[]{:S(2)}) %collective-permute-start.18) | collective-permute-done | bytes 1048608 | tf_op jit(solution)/shard_map/ppermute | solution.py:79
  34.2 1.6 collective-permute-start.17
  36.8 4.4 %maximum_select_fusion = bf16[1024,1024]{1,0:T(8,128)(2,1)} fusion(bf16[1024,512]{1,0:T(8,128)(2,1)} %collective-permute-done.5, bf16[1024,512]{1,0:T(8,128)(2,1)} %param.5, pred[]{:T(512)S(6)} %eq.44), kind=kLoop, calls=%fused_computation.7 | loop fusion | flops 9437184 | bytes 4194305 | tf_op jit(solution)/shard_map/jit(_where)/select_n | solution.py:355
  41.2 14.0 %collective-permute-done.3.refs_2_.refs_1_ = bf16[2048,256]{1,0:T(8,128)(2,1)} collective-permute-done((bf16[2048,256]{1,0:T(8,128)(2,1)S(1)}, bf16[2048,256]{1,0:T(8,128)(2,1)}, u32[]{:S(2)}, u32[]{:S(2)}) %collective-permute-start.3) | collective-permute-done | bytes 1048608 | tf_op jit(solution)/shard_map/ppermute | solution.py:79
  58.2 19.5 %collective-permute-done.19 = bf16[2048,256]{1,0:T(8,128)(2,1)} collective-permute-done((bf16[2048,256]{1,0:T(8,128)(2,1)S(1)}, bf16[2048,256]{1,0:T(8,128)(2,1)}, u32[]{:S(2)}, u32[]{:S(2)}) %collective-permute-start.19) | collective-permute-done | bytes 1048608 | tf_op jit(solution)/shard_map/ppermute | solution.py:79
  80.4 19.8 %collective-permute-done.4 = bf16[2048,256]{1,0:T(8,128)(2,1)} collective-permute-done((bf16[2048,256]{1,0:T(8,128)(2,1)}, bf16[2048,256]{1,0:T(8,128)(2,1)}, u32[]{:S(2)}, u32[]{:S(2)}) %collective-permute-start.4) | collective-permute-done | bytes 1048608 | tf_op jit(solution)/shard_map/ppermute | solution.py:79
  102.9 2.7 pad_maximum_fusion.refs_3_.refs_2_.refs_1_
  105.5 2.0 token_product.10
  108.9 2.0 token_product.14
  112.2 3.6 %token_product.9 = f32[256,1024]{1,0:T(8,128)S(1)} custom-call(bf16[2048,256]{1,0:T(8,128)(2,1)} %collective-permute-done.1.refs_1_.refs_0_, bf16[2048,256]{1,0:T(8,128)(2,1)} %collective-permute-done.3.refs_2_.refs_1_, bf16[2048,1024]{1,0:T(8,128)(2,1)S(1)} %pad_maximum_fusion.refs_3_.refs_2_.refs_1_), custom_call_target="tpu_custom_call" | custom-call | flops 1073741824 | bytes 6291456 | tf_op jit(solution)/shard_map/token_product/pallas_call | solution.py:126
  117.2 3.6 %token_product.8 = f32[256,1024]{1,0:T(8,128)S(1)} custom-call(bf16[2048,256]{1,0:T(8,128)(2,1)S(1)} %broadcast_select_fusion.2.refs_0_.refs_1_, bf16[2048,256]{1,0:T(8,128)(2,1)} %collective-permute-done.1.refs_1_.refs_0_, bf16[2048,256]{1,0:T(8,128)(2,1)} %collective-permute-done.3.refs_2_.refs_1_, ...), custom_call_target="tpu_custom_call" | custom-call | flops 1073741824 | bytes 6291456 | tf_op jit(solution)/shard_map/token_product/pallas_call | solution.py:126
  120.9 1.7 collective-permute-done.24.refs_0_
  122.6 3.9 %collective-permute-start.7 = (f32[256,1024]{1,0:T(8,128)S(1)}, f32[256,1024]{1,0:T(8,128)S(1)}, u32[]{:S(2)}, u32[]{:S(2)}) collective-permute-start(f32[256,1024]{1,0:T(8,128)S(1)} %token_product.8), channel_id=1, source_target_pairs={{0,16},{1,17},{4,20},{5,21},{8,24},{9,25},{12,28},{13,29},{18,2},{... | collective-permute-start | bytes 3145736 | tf_op jit(solution)/shard_map/ppermute | solution.py:79
  126.5 4.3 %token_product.12 = f32[256,1024]{1,0:T(8,128)} custom-call(bf16[2048,256]{1,0:T(8,128)(2,1)S(1)} %broadcast_select_fusion.1.refs_0_.refs_1_, bf16[2048,256]{1,0:T(8,128)(2,1)} %collective-permute-done.16.refs_1_.refs_0_, bf16[2048,256]{1,0:T(8,128)(2,1)S(1)} %copy-done.7, bf16[2048,1024]{1,0:T(8,128)(2,1)S(1)} %pad_maximum_fusion.refs_3_.refs_2_.refs_1_), custom_call_target="tpu_custom_call" | custom-call | flops 1073741824 | bytes 6291456 | tf_op jit(solution)/shard_map/token_product/pallas_call | solution.py:126
  130.8 3.3 %token_product.13 = f32[256,1024]{1,0:T(8,128)S(1)} custom-call(bf16[2048,256]{1,0:T(8,128)(2,1)} %collective-permute-done.16.refs_1_.refs_0_, bf16[2048,256]{1,0:T(8,128)(2,1)S(1)} %copy-done.7, bf16[2048,1024]{1,0:T(8,128)(2,1)S(1)} %pad_maximum_fusion.refs_3_.refs_2_.refs_1_), custom_call_target="tpu_custom_call" | custom-call | flops 1073741824 | bytes 6291456 | tf_op jit(solution)/shard_map/token_product/pallas_call | solution.py:126
  134.1 10.4 %collective-permute-done.11.refs_0_ = bf16[2048,256]{1,0:T(8,128)(2,1)S(1)} collective-permute-done((bf16[2048,256]{1,0:T(8,128)(2,1)S(1)}, bf16[2048,256]{1,0:T(8,128)(2,1)S(1)}, u32[]{:S(2)}, u32[]{:S(2)}) %collective-permute-start.11) | collective-permute-done | bytes 1048608 | tf_op jit(solution)/shard_map/ppermute | solution.py:79
  145.8 6.5 %collective-permute-start.20 = (f32[256,1024]{1,0:T(8,128)}, f32[256,1024]{1,0:T(8,128)}, u32[]{:S(2)}, u32[]{:S(2)}) collective-permute-start(f32[256,1024]{1,0:T(8,128)} %token_product.12), channel_id=1, source_target_pairs={{0,16},{1,17},{4,20},{5,21},{8,24},{9,25},{12,28},{13,29},{18,2},{... | collective-permute-start | bytes 3145736 | tf_op jit(solution)/shard_map/ppermute | solution.py:79
  152.3 2.3 token_product.11.refs_2_
  154.6 3.3 %collective-permute-done.22 = f32[256,1024]{1,0:T(8,128)S(1)} collective-permute-done((f32[256,1024]{1,0:T(8,128)S(1)}, f32[256,1024]{1,0:T(8,128)S(1)}, u32[]{:S(2)}, u32[]{:S(2)}) %collective-permute-start.22) | collective-permute-done | bytes 1048608 | tf_op jit(solution)/shard_map/ppermute | solution.py:79
  158.0 1.7 collective-permute-start.14
  159.6 20.8 %collective-permute-done.8 = f32[256,1024]{1,0:T(8,128)S(1)} collective-permute-done((f32[256,1024]{1,0:T(8,128)S(1)}, f32[256,1024]{1,0:T(8,128)S(1)}, u32[]{:S(2)}, u32[]{:S(2)}) %collective-permute-start.8) | collective-permute-done | bytes 1048608 | tf_op jit(solution)/shard_map/ppermute | solution.py:79
  180.4 2.2 collective-permute-start.13
  185.3 2.2 copy-done.1
  191.2 1.7 select_select_fusion.2
  192.9 8.1 %collective-permute-done.21 = f32[256,1024]{1,0:T(8,128)} collective-permute-done((f32[256,1024]{1,0:T(8,128)S(1)}, f32[256,1024]{1,0:T(8,128)}, u32[]{:S(2)}, u32[]{:S(2)}) %collective-permute-start.21) | collective-permute-done | bytes 1048608 | tf_op jit(solution)/shard_map/ppermute | solution.py:79
  201.9 2.6 select_select_fusion
  204.5 2.1 collective-permute-start.26
  208.3 5.4 %fusion = (bf16[1024,1024]{1,0:T(8,128)(2,1)S(1)}, bf16[1024,1024]{1,0:T(8,128)(2,1)S(1)}, bf16[1024,1024]{1,0:T(8,128)(2,1)S(1)}, bf16[1024,1024]{1,0:T(8,128)(2,1)S(1)}) fusion(f32[1,1024,1024]{2,1,0:T(8,128)} %param.6, f32[1,1024,1024]{2,1,0:T(8,128)} %param.7), kind=kLoop, calls=%fused_computation.4 | loop fusion | flops 8388608 | bytes 16777216 | tf_op jit(solution)/shard_map/convert_element_type | solution.py:149
  213.7 9.5 %advance.2 = (f32[1024,1024]{1,0:T(8,128)S(1)}, f32[1]{0:T(128)}) custom-call(f32[1]{0:T(128)} %constant.46.clone.1.squares_ref, f32[256,1024]{1,0:T(8,128)S(1)} %get-tuple-element.16.refs_0_, f32[256,1024]{1,0:T(8,128)S(1)} %collective-permute-done.10.refs_1_, f32[256,1024]{1,0:T(8,128)} %token_product.11.refs_2_, ...), custom_call_target="tpu_custom_call" | custom-call | flops 6442450944 | bytes 20971520 | tf_op jit(solution)/shard_map/advance/pallas_call | solution.py:242
  223.1 6.2 %collective-permute-done.26.refs_4_ = f32[256,1024]{1,0:T(8,128)S(1)} collective-permute-done((f32[256,1024]{1,0:T(8,128)S(1)}, f32[256,1024]{1,0:T(8,128)S(1)}, u32[]{:S(2)}, u32[]{:S(2)}) %collective-permute-start.26) | collective-permute-done | bytes 1048608 | tf_op jit(solution)/shard_map/ppermute | solution.py:79
  229.3 9.1 %finish.2 = (bf16[1024,512]{1,0:T(8,128)(2,1)S(1)}, bf16[512,512]{1,0:T(8,128)(2,1)}, bf16[512,512]{1,0:T(8,128)(2,1)}) custom-call(f32[1]{0:T(128)} %get-tuple-element.18.squares_ref, f32[256,1024]{1,0:T(8,128)S(1)} %get-tuple-element.19.refs_0_, f32[256,1024]{1,0:T(8,128)S(1)} %collective-permute-done.23.refs_1_, f32[256,1024]{1,0:T(8,128)S(1)} %token_product.15.refs_2_, ...), custom_call_target="tpu_custom_call" | custom-call | flops 6442450944 | bytes 20971520 | tf_op jit(solution)/shard_map/finish/pallas_call | solution.py:242
  238.4 1.7 collective-permute-start.37
  240.1 9.1 %advance.3 = (f32[1024,1024]{1,0:T(8,128)S(1)}, f32[1]{0:T(128)}) custom-call(f32[1]{0:T(128)} %constant.46.clone.1.squares_ref, f32[256,1024]{1,0:T(8,128)S(1)} %get-tuple-element.16.refs_0_, f32[256,1024]{1,0:T(8,128)S(1)} %collective-permute-done.10.refs_1_, bf16[1024,1024]{1,0:T(8,128)(2,1)S(1)} %get-tuple-element.34.refs_6_.refs_2_, ...), custom_call_target="tpu_custom_call" | custom-call | flops 6442450944 | bytes 20971520 | tf_op jit(solution)/shard_map/advance/pallas_call | solution.py:242
  249.2 7.8 %finish.3 = bf16[1024,512]{1,0:T(8,128)(2,1)S(1)} custom-call(f32[1]{0:T(128)} %get-tuple-element.25.squares_ref, f32[256,1024]{1,0:T(8,128)S(1)} %get-tuple-element.19.refs_0_, f32[256,1024]{1,0:T(8,128)S(1)} %collective-permute-done.23.refs_1_, bf16[1024,1024]{1,0:T(8,128)(2,1)S(1)} %get-tuple-element.34.refs_6_.refs_2_, ...), custom_call_target="tpu_custom_call" | custom-call | flops 6442450944 | bytes 20971520 | tf_op jit(solution)/shard_map/finish/pallas_call | solution.py:242
  257.0 1.9 collective-permute-start.38
  261.0 3.9 %collective-permute-start.34 = (bf16[1024,512]{1,0:T(8,128)(2,1)S(1)}, bf16[1024,512]{1,0:T(8,128)(2,1)S(1)}, u32[]{:S(2)}, u32[]{:S(2)}) collective-permute-start(bf16[1024,512]{1,0:T(8,128)(2,1)S(1)} %get-tuple-element.24.refs_0_), channel_id=1, source_target_pairs={{0,8},{1,9},{2,10},{3,11},{4,12},{5,13},{6,14},{7,15},{8,0},{9,1},... | collective-permute-start | bytes 3145736 | tf_op jit(solution)/shard_map/ppermute | solution.py:79
  265.0 5.6 %collective-permute-done.28.refs_4_ = bf16[512,512]{1,0:T(8,128)(2,1)S(1)} collective-permute-done((bf16[512,512]{1,0:T(8,128)(2,1)}, bf16[512,512]{1,0:T(8,128)(2,1)S(1)}, u32[]{:S(2)}, u32[]{:S(2)}) %collective-permute-start.28) | collective-permute-done | bytes 524320 | tf_op jit(solution)/shard_map/ppermute | solution.py:79
  270.5 7.1 %collective-permute-start.36 = (bf16[512,512]{1,0:T(8,128)(2,1)S(1)}, bf16[512,512]{1,0:T(8,128)(2,1)S(1)}, u32[]{:S(2)}, u32[]{:S(2)}) collective-permute-start(bf16[512,512]{1,0:T(8,128)(2,1)S(1)} %collective-permute-done.28.refs_4_), channel_id=1, source_target_pairs={{0,8},{1,9},{2,10},{3,11},{4,12},{5,13},{6,14},{7,15},{8,0},{9,1},... | collective-permute-start | bytes 1572872 | tf_op jit(solution)/shard_map/ppermute | solution.py:79
  277.7 2.0 collective-permute-done.38
  281.0 3.0 collective-permute-start.39
  284.0 3.0 collective-permute-start.32
  287.1 12.7 %collective-permute-done.32.refs_0_ = bf16[512,512]{1,0:T(8,128)(2,1)S(1)} collective-permute-done((bf16[512,512]{1,0:T(8,128)(2,1)S(1)}, bf16[512,512]{1,0:T(8,128)(2,1)S(1)}, u32[]{:S(2)}, u32[]{:S(2)}) %collective-permute-start.32) | collective-permute-done | bytes 524320 | tf_op jit(solution)/shard_map/ppermute | solution.py:79
  299.8 10.7 %collective-permute-done.29.refs_0_ = bf16[512,512]{1,0:T(8,128)(2,1)S(1)} collective-permute-done((bf16[512,512]{1,0:T(8,128)(2,1)S(1)}, bf16[512,512]{1,0:T(8,128)(2,1)S(1)}, u32[]{:S(2)}, u32[]{:S(2)}) %collective-permute-start.29) | collective-permute-done | bytes 524320 | tf_op jit(solution)/shard_map/ppermute | solution.py:79
  310.5 2.8 put.3.refs_2_
  (98 shorter events, 35.1 us)
Async XLA Ops:
  1.7 2.1 collective-permute-start.15
  2.2 11.3 %collective-permute-start = (bf16[1024,256]{1,0:T(8,128)(2,1)S(1)}, bf16[1024,256]{1,0:T(8,128)(2,1)S(1)}, u32[]{:S(2)}, u32[]{:S(2)}) collective-permute-start(bf16[1024,256]{1,0:T(8,128)(2,1)S(1)} %get-tuple-element.36), channel_id=1, source_target_pairs={{0,8},{1,9},{2,10},{3,11},{4,12},{5,13},{6,14},{7,15},{8,0},{9,1},... | collective-permute-start | bytes 1572872 | tf_op jit(solution)/shard_map/ppermute | solution.py:79
  3.8 28.8 %collective-permute-start.18 = (bf16[2048,256]{1,0:T(8,128)(2,1)S(1)}, bf16[2048,256]{1,0:T(8,128)(2,1)S(1)}, u32[]{:S(2)}, u32[]{:S(2)}) collective-permute-start(bf16[2048,256]{1,0:T(8,128)(2,1)S(1)} %pad_maximum_fusion.2.refs_0_), channel_id=1, source_target_pairs={{2,0},{3,1},{4,2},{5,3},{6,4},{7,5},{10,8},{11,9},{12,10},{13,11},... | collective-permute-start | bytes 3145736 | tf_op jit(solution)/shard_map/ppermute | solution.py:79
  5.1 29.0 %collective-permute-start.16 = (bf16[2048,256]{1,0:T(8,128)(2,1)S(1)}, bf16[2048,256]{1,0:T(8,128)(2,1)}, u32[]{:S(2)}, u32[]{:S(2)}) collective-permute-start(bf16[2048,256]{1,0:T(8,128)(2,1)S(1)} %pad_maximum_fusion.2.refs_0_), channel_id=1, source_target_pairs={{0,2},{1,3},{2,4},{3,5},{4,6},{5,7},{8,10},{9,11},{10,12},{11,13},... | collective-permute-start | bytes 3145736 | tf_op jit(solution)/shard_map/ppermute | solution.py:79
  11.6 25.2 %collective-permute-start.5 = (bf16[1024,512]{1,0:T(8,128)(2,1)}, bf16[1024,512]{1,0:T(8,128)(2,1)}, u32[]{:S(2)}, u32[]{:S(2)}) collective-permute-start(bf16[1024,512]{1,0:T(8,128)(2,1)} %param.5), channel_id=1, source_target_pairs={{0,1},{1,0},{2,3},{3,2},{4,5},{5,4},{6,7},{7,6},{8,9},{9,8},{10,11... | collective-permute-start | bytes 3145736 | tf_op jit(solution)/shard_map/ppermute | solution.py:79
  13.6 41.6 %collective-permute-start.3 = (bf16[2048,256]{1,0:T(8,128)(2,1)S(1)}, bf16[2048,256]{1,0:T(8,128)(2,1)}, u32[]{:S(2)}, u32[]{:S(2)}) collective-permute-start(bf16[2048,256]{1,0:T(8,128)(2,1)S(1)} %pad_maximum_fusion.1.refs_0_), channel_id=1, source_target_pairs={{2,0},{3,1},{4,2},{5,3},{6,4},{7,5},{10,8},{11,9},{12,10},{13,11},... | collective-permute-start | bytes 3145736 | tf_op jit(solution)/shard_map/ppermute | solution.py:79
  14.9 41.6 %collective-permute-start.1 = (bf16[2048,256]{1,0:T(8,128)(2,1)S(1)}, bf16[2048,256]{1,0:T(8,128)(2,1)}, u32[]{:S(2)}, u32[]{:S(2)}) collective-permute-start(bf16[2048,256]{1,0:T(8,128)(2,1)S(1)} %pad_maximum_fusion.1.refs_0_), channel_id=1, source_target_pairs={{0,2},{1,3},{2,4},{3,5},{4,6},{5,7},{8,10},{9,11},{10,12},{11,13},... | collective-permute-start | bytes 3145736 | tf_op jit(solution)/shard_map/ppermute | solution.py:79
  32.7 8.5 %copy-start.6 = (bf16[2048,256]{1,0:T(8,128)(2,1)}, bf16[2048,256]{1,0:T(8,128)(2,1)S(1)}, u32[]{:S(2)}) copy-start(bf16[2048,256]{1,0:T(8,128)(2,1)S(1)} %collective-permute-done.18.refs_2_.refs_1_) | copy-start | bytes 3145732
  32.7 45.0 %collective-permute-start.19 = (bf16[2048,256]{1,0:T(8,128)(2,1)S(1)}, bf16[2048,256]{1,0:T(8,128)(2,1)}, u32[]{:S(2)}, u32[]{:S(2)}) collective-permute-start(bf16[2048,256]{1,0:T(8,128)(2,1)S(1)} %collective-permute-done.18.refs_2_.refs_1_), channel_id=1, source_target_pairs={{2,0},{3,1},{4,2},{5,3},{10,8},{11,9},{12,10},{13,11},{18,16},{19,... | collective-permute-start | bytes 3145736 | tf_op jit(solution)/shard_map/ppermute | solution.py:79
  34.2 43.6 %collective-permute-start.17 = (bf16[2048,256]{1,0:T(8,128)(2,1)}, bf16[2048,256]{1,0:T(8,128)(2,1)}, u32[]{:S(2)}, u32[]{:S(2)}) collective-permute-start(bf16[2048,256]{1,0:T(8,128)(2,1)} %collective-permute-done.16.refs_1_.refs_0_), channel_id=1, source_target_pairs={{2,4},{3,5},{4,6},{5,7},{10,12},{11,13},{12,14},{13,15},{18,20},{1... | collective-permute-start | bytes 3145736 | tf_op jit(solution)/shard_map/ppermute | solution.py:79
  41.2 61.6 %collective-permute-start.6 = (bf16[1024,1024]{1,0:T(8,128)(2,1)}, bf16[1024,1024]{1,0:T(8,128)(2,1)}, u32[]{:S(2)}, u32[]{:S(2)}) collective-permute-start(bf16[1024,1024]{1,0:T(8,128)(2,1)} %maximum_select_fusion), channel_id=1, source_target_pairs={{0,8},{1,9},{2,10},{3,11},{4,12},{5,13},{6,14},{7,15},{8,0},{9,1},... | collective-permute-start | bytes 6291464 | tf_op jit(solution)/shard_map/ppermute | solution.py:79
  55.3 44.9 %collective-permute-start.4 = (bf16[2048,256]{1,0:T(8,128)(2,1)}, bf16[2048,256]{1,0:T(8,128)(2,1)}, u32[]{:S(2)}, u32[]{:S(2)}) collective-permute-start(bf16[2048,256]{1,0:T(8,128)(2,1)} %collective-permute-done.3.refs_2_.refs_1_), channel_id=1, source_target_pairs={{2,0},{3,1},{4,2},{5,3},{10,8},{11,9},{12,10},{13,11},{18,16},{19,... | collective-permute-start | bytes 3145736 | tf_op jit(solution)/shard_map/ppermute | solution.py:79
  56.6 43.6 %collective-permute-start.2 = (bf16[2048,256]{1,0:T(8,128)(2,1)}, bf16[2048,256]{1,0:T(8,128)(2,1)}, u32[]{:S(2)}, u32[]{:S(2)}) collective-permute-start(bf16[2048,256]{1,0:T(8,128)(2,1)} %collective-permute-done.1.refs_1_.refs_0_), channel_id=1, source_target_pairs={{2,4},{3,5},{4,6},{5,7},{10,12},{11,13},{12,14},{13,15},{18,20},{1... | collective-permute-start | bytes 3145736 | tf_op jit(solution)/shard_map/ppermute | solution.py:79
  79.1 43.5 %collective-permute-start.24 = (bf16[2048,256]{1,0:T(8,128)(2,1)S(1)}, bf16[2048,256]{1,0:T(8,128)(2,1)S(1)}, u32[]{:S(2)}, u32[]{:S(2)}) collective-permute-start(bf16[2048,256]{1,0:T(8,128)(2,1)S(1)} %broadcast_select_fusion.1.refs_0_.refs_1_), channel_id=1, source_target_pairs={{2,0},{3,1},{4,6},{5,7},{10,8},{11,9},{12,14},{13,15},{18,16},{19,... | collective-permute-start | bytes 3145736 | tf_op jit(solution)/shard_map/ppermute | solution.py:79
  101.6 42.9 %collective-permute-start.11 = (bf16[2048,256]{1,0:T(8,128)(2,1)S(1)}, bf16[2048,256]{1,0:T(8,128)(2,1)S(1)}, u32[]{:S(2)}, u32[]{:S(2)}) collective-permute-start(bf16[2048,256]{1,0:T(8,128)(2,1)S(1)} %broadcast_select_fusion.2.refs_0_.refs_1_), channel_id=1, source_target_pairs={{2,0},{3,1},{4,6},{5,7},{10,8},{11,9},{12,14},{13,15},{18,16},{19,... | collective-permute-start | bytes 3145736 | tf_op jit(solution)/shard_map/ppermute | solution.py:79
  105.5 46.8 %copy-start = (bf16[2048,1024]{1,0:T(8,128)(2,1)}, bf16[2048,1024]{1,0:T(8,128)(2,1)S(1)}, u32[]{:S(2)}) copy-start(bf16[2048,1024]{1,0:T(8,128)(2,1)S(1)} %pad_maximum_fusion.refs_3_.refs_2_.refs_1_) | copy-start | bytes 12582916
  107.6 38.2 %collective-permute-start.9 = (f32[256,1024]{1,0:T(8,128)S(1)}, f32[256,1024]{1,0:T(8,128)S(1)}, u32[]{:S(2)}, u32[]{:S(2)}) collective-permute-start(f32[256,1024]{1,0:T(8,128)S(1)} %token_product.10), channel_id=1, source_target_pairs={{4,20},{5,21},{6,22},{7,23},{12,28},{13,29},{14,30},{15,31},{16,0}... | collective-permute-start | bytes 3145736 | tf_op jit(solution)/shard_map/ppermute | solution.py:79
  110.9 47.1 %collective-permute-start.22 = (f32[256,1024]{1,0:T(8,128)S(1)}, f32[256,1024]{1,0:T(8,128)S(1)}, u32[]{:S(2)}, u32[]{:S(2)}) collective-permute-start(f32[256,1024]{1,0:T(8,128)S(1)} %token_product.14), channel_id=1, source_target_pairs={{4,20},{5,21},{6,22},{7,23},{12,28},{13,29},{14,30},{15,31},{16,0}... | collective-permute-start | bytes 3145736 | tf_op jit(solution)/shard_map/ppermute | solution.py:79
  115.8 10.7 %copy-start.7 = (bf16[2048,256]{1,0:T(8,128)(2,1)S(1)}, bf16[2048,256]{1,0:T(8,128)(2,1)}, u32[]{:S(2)}) copy-start(bf16[2048,256]{1,0:T(8,128)(2,1)} %copy-done.6) | copy-start | bytes 3145732
  115.8 64.6 %collective-permute-start.8 = (f32[256,1024]{1,0:T(8,128)S(1)}, f32[256,1024]{1,0:T(8,128)S(1)}, u32[]{:S(2)}, u32[]{:S(2)}) collective-permute-start(f32[256,1024]{1,0:T(8,128)S(1)} %token_product.9), channel_id=1, source_target_pairs={{2,18},{3,19},{6,22},{7,23},{10,26},{11,27},{14,30},{15,31},{16,0}... | collective-permute-start | bytes 3145736 | tf_op jit(solution)/shard_map/ppermute | solution.py:79
  120.9 9.9 %copy-start.8 = (f32[256,1024]{1,0:T(8,128)}, f32[256,1024]{1,0:T(8,128)S(1)}, u32[]{:S(2)}) copy-start(f32[256,1024]{1,0:T(8,128)S(1)} %token_product.8) | copy-start | bytes 3145732
  122.6 60.1 %collective-permute-start.7 = (f32[256,1024]{1,0:T(8,128)S(1)}, f32[256,1024]{1,0:T(8,128)S(1)}, u32[]{:S(2)}, u32[]{:S(2)}) collective-permute-start(f32[256,1024]{1,0:T(8,128)S(1)} %token_product.8), channel_id=1, source_target_pairs={{0,16},{1,17},{4,20},{5,21},{8,24},{9,25},{12,28},{13,29},{18,2},{... | collective-permute-start | bytes 3145736 | tf_op jit(solution)/shard_map/ppermute | solution.py:79
  144.5 56.5 %collective-permute-start.21 = (f32[256,1024]{1,0:T(8,128)S(1)}, f32[256,1024]{1,0:T(8,128)}, u32[]{:S(2)}, u32[]{:S(2)}) collective-permute-start(f32[256,1024]{1,0:T(8,128)S(1)} %token_product.13), channel_id=1, source_target_pairs={{2,18},{3,19},{6,22},{7,23},{10,26},{11,27},{14,30},{15,31},{16,0}... | collective-permute-start | bytes 3145736 | tf_op jit(solution)/shard_map/ppermute | solution.py:79
  145.8 8.8 %copy-start.14 = (f32[256,1024]{1,0:T(8,128)}, f32[256,1024]{1,0:T(8,128)S(1)}, u32[]{:S(2)}) copy-start(f32[256,1024]{1,0:T(8,128)S(1)} %collective-permute-done.9) | copy-start | bytes 3145732
  145.8 56.0 %collective-permute-start.20 = (f32[256,1024]{1,0:T(8,128)}, f32[256,1024]{1,0:T(8,128)}, u32[]{:S(2)}, u32[]{:S(2)}) collective-permute-start(f32[256,1024]{1,0:T(8,128)} %token_product.12), channel_id=1, source_target_pairs={{0,16},{1,17},{4,20},{5,21},{8,24},{9,25},{12,28},{13,29},{18,2},{... | collective-permute-start | bytes 3145736 | tf_op jit(solution)/shard_map/ppermute | solution.py:79
  158.0 24.7 %copy-start.12 = (f32[256,1024]{1,0:T(8,128)}, f32[256,1024]{1,0:T(8,128)S(1)}, u32[]{:S(2)}) copy-start(f32[256,1024]{1,0:T(8,128)S(1)} %collective-permute-done.22) | copy-start | bytes 3145732
  158.0 46.5 %collective-permute-start.14 = (f32[256,1024]{1,0:T(8,128)}, f32[256,1024]{1,0:T(8,128)}, u32[]{:S(2)}, u32[]{:S(2)}) collective-permute-start(f32[256,1024]{1,0:T(8,128)} %token_product.11.refs_2_), channel_id=1, source_target_pairs={{12,4},{13,5},{14,6},{15,7},{16,24},{17,25},{18,26},{19,27}} | collective-permute-start | bytes 3145736 | tf_op jit(solution)/shard_map/ppermute | solution.py:79
  180.4 26.2 %collective-permute-start.13 = (f32[256,1024]{1,0:T(8,128)}, f32[256,1024]{1,0:T(8,128)}, u32[]{:S(2)}, u32[]{:S(2)}) collective-permute-start(f32[256,1024]{1,0:T(8,128)} %token_product.11.refs_2_), channel_id=1, source_target_pairs={{0,24},{1,25},{2,26},{3,27},{28,4},{29,5},{30,6},{31,7}} | collective-permute-start | bytes 3145736 | tf_op jit(solution)/shard_map/ppermute | solution.py:79
  183.7 23.9 %collective-permute-start.12 = (f32[256,1024]{1,0:T(8,128)}, f32[256,1024]{1,0:T(8,128)}, u32[]{:S(2)}, u32[]{:S(2)}) collective-permute-start(f32[256,1024]{1,0:T(8,128)} %token_product.11.refs_2_), channel_id=1, source_target_pairs={{8,24},{9,25},{10,26},{11,27},{20,4},{21,5},{22,6},{23,7}} | collective-permute-start | bytes 3145736 | tf_op jit(solution)/shard_map/ppermute | solution.py:79
  191.2 10.7 %copy-start.3 = (f32[256,1024]{1,0:T(8,128)S(1)}, f32[256,1024]{1,0:T(8,128)}, u32[]{:S(2)}) copy-start(f32[256,1024]{1,0:T(8,128)} %copy-done.2) | copy-start | bytes 3145732
  191.2 10.7 %copy-start.13 = (f32[256,1024]{1,0:T(8,128)S(1)}, f32[256,1024]{1,0:T(8,128)}, u32[]{:S(2)}) copy-start(f32[256,1024]{1,0:T(8,128)} %copy-done.12) | copy-start | bytes 3145732
  201.0 22.1 %collective-permute-start.27 = (f32[256,1024]{1,0:T(8,128)S(1)}, f32[256,1024]{1,0:T(8,128)S(1)}, u32[]{:S(2)}, u32[]{:S(2)}) collective-permute-start(f32[256,1024]{1,0:T(8,128)S(1)} %token_product.15.refs_2_), channel_id=1, source_target_pairs={{12,4},{13,5},{14,6},{15,7},{16,24},{17,25},{18,26},{19,27}} | collective-permute-start | bytes 3145736 | tf_op jit(solution)/shard_map/ppermute | solution.py:79
  201.8 11.9 %collective-permute-start.10 = (f32[256,1024]{1,0:T(8,128)}, f32[256,1024]{1,0:T(8,128)S(1)}, u32[]{:S(2)}, u32[]{:S(2)}) collective-permute-start(f32[256,1024]{1,0:T(8,128)} %get-tuple-element.17), channel_id=1, source_target_pairs={{0,8},{1,9},{2,10},{3,11},{4,12},{5,13},{6,14},{7,15},{8,0},{9,1},... | collective-permute-start | bytes 3145736 | tf_op jit(solution)/shard_map/ppermute | solution.py:79
  204.5 24.9 %collective-permute-start.26 = (f32[256,1024]{1,0:T(8,128)S(1)}, f32[256,1024]{1,0:T(8,128)S(1)}, u32[]{:S(2)}, u32[]{:S(2)}) collective-permute-start(f32[256,1024]{1,0:T(8,128)S(1)} %token_product.15.refs_2_), channel_id=1, source_target_pairs={{0,24},{1,25},{2,26},{3,27},{28,4},{29,5},{30,6},{31,7}} | collective-permute-start | bytes 3145736 | tf_op jit(solution)/shard_map/ppermute | solution.py:79
  206.6 22.7 %collective-permute-start.25 = (f32[256,1024]{1,0:T(8,128)S(1)}, f32[256,1024]{1,0:T(8,128)S(1)}, u32[]{:S(2)}, u32[]{:S(2)}) collective-permute-start(f32[256,1024]{1,0:T(8,128)S(1)} %token_product.15.refs_2_), channel_id=1, source_target_pairs={{8,24},{9,25},{10,26},{11,27},{20,4},{21,5},{22,6},{23,7}} | collective-permute-start | bytes 3145736 | tf_op jit(solution)/shard_map/ppermute | solution.py:79
  207.5 21.8 %collective-permute-start.23 = (f32[256,1024]{1,0:T(8,128)S(1)}, f32[256,1024]{1,0:T(8,128)S(1)}, u32[]{:S(2)}, u32[]{:S(2)}) collective-permute-start(f32[256,1024]{1,0:T(8,128)S(1)} %get-tuple-element.20), channel_id=1, source_target_pairs={{0,8},{1,9},{2,10},{3,11},{4,12},{5,13},{6,14},{7,15},{8,0},{9,1},... | collective-permute-start | bytes 3145736 | tf_op jit(solution)/shard_map/ppermute | solution.py:79
  238.4 39.2 %collective-permute-start.37 = (bf16[1024,512]{1,0:T(8,128)(2,1)S(1)}, bf16[1024,512]{1,0:T(8,128)(2,1)}, u32[]{:S(2)}, u32[]{:S(2)}) collective-permute-start(bf16[1024,512]{1,0:T(8,128)(2,1)S(1)} %get-tuple-element.24.refs_0_), channel_id=1, source_target_pairs={{4,20},{5,21},{6,22},{7,23},{24,8},{25,9},{26,10},{27,11}} | collective-permute-start | bytes 3145736 | tf_op jit(solution)/shard_map/ppermute | solution.py:79
  257.0 22.6 %collective-permute-start.38 = (bf16[1024,512]{1,0:T(8,128)(2,1)S(1)}, bf16[1024,512]{1,0:T(8,128)(2,1)}, u32[]{:S(2)}, u32[]{:S(2)}) collective-permute-start(bf16[1024,512]{1,0:T(8,128)(2,1)S(1)} %finish.3), channel_id=1, source_target_pairs={{0,16},{1,17},{2,18},{3,19},{8,24},{9,25},{10,26},{11,27},{12,28},... | collective-permute-start | bytes 3145736 | tf_op jit(solution)/shard_map/ppermute | solution.py:79
  259.0 11.6 %collective-permute-start.28 = (bf16[512,512]{1,0:T(8,128)(2,1)}, bf16[512,512]{1,0:T(8,128)(2,1)S(1)}, u32[]{:S(2)}, u32[]{:S(2)}) collective-permute-start(bf16[512,512]{1,0:T(8,128)(2,1)} %get-tuple-element.22), channel_id=1, source_target_pairs={{0,1},{1,0},{2,3},{3,2},{4,5},{5,4},{6,7},{7,6},{8,9},{9,8},{10,11... | collective-permute-start | bytes 1572872 | tf_op jit(solution)/shard_map/ppermute | solution.py:79
  260.4 23.6 %collective-permute-start.31 = (bf16[512,512]{1,0:T(8,128)(2,1)}, bf16[512,512]{1,0:T(8,128)(2,1)S(1)}, u32[]{:S(2)}, u32[]{:S(2)}) collective-permute-start(bf16[512,512]{1,0:T(8,128)(2,1)} %get-tuple-element.23), channel_id=1, source_target_pairs={{0,1},{1,0},{2,3},{3,2},{4,5},{5,4},{6,7},{7,6},{8,9},{9,8},{10,11... | collective-permute-start | bytes 1572872 | tf_op jit(solution)/shard_map/ppermute | solution.py:79
  261.0 49.4 %collective-permute-start.34 = (bf16[1024,512]{1,0:T(8,128)(2,1)S(1)}, bf16[1024,512]{1,0:T(8,128)(2,1)S(1)}, u32[]{:S(2)}, u32[]{:S(2)}) collective-permute-start(bf16[1024,512]{1,0:T(8,128)(2,1)S(1)} %get-tuple-element.24.refs_0_), channel_id=1, source_target_pairs={{0,8},{1,9},{2,10},{3,11},{4,12},{5,13},{6,14},{7,15},{8,0},{9,1},... | collective-permute-start | bytes 3145736 | tf_op jit(solution)/shard_map/ppermute | solution.py:79
  270.5 16.6 %collective-permute-start.36 = (bf16[512,512]{1,0:T(8,128)(2,1)S(1)}, bf16[512,512]{1,0:T(8,128)(2,1)S(1)}, u32[]{:S(2)}, u32[]{:S(2)}) collective-permute-start(bf16[512,512]{1,0:T(8,128)(2,1)S(1)} %collective-permute-done.28.refs_4_), channel_id=1, source_target_pairs={{0,8},{1,9},{2,10},{3,11},{4,12},{5,13},{6,14},{7,15},{8,0},{9,1},... | collective-permute-start | bytes 1572872 | tf_op jit(solution)/shard_map/ppermute | solution.py:79
  281.0 29.5 %collective-permute-start.39 = (bf16[1024,512]{1,0:T(8,128)(2,1)S(1)}, bf16[1024,512]{1,0:T(8,128)(2,1)S(1)}, u32[]{:S(2)}, u32[]{:S(2)}) collective-permute-start(bf16[1024,512]{1,0:T(8,128)(2,1)S(1)} %broadcast_select_fusion.refs_6_), channel_id=1, source_target_pairs={{0,8},{1,9},{2,10},{3,11},{4,12},{5,13},{6,14},{7,15},{8,0},{9,1},... | collective-permute-start | bytes 3145736 | tf_op jit(solution)/shard_map/ppermute | solution.py:79
  284.0 15.8 %collective-permute-start.32 = (bf16[512,512]{1,0:T(8,128)(2,1)S(1)}, bf16[512,512]{1,0:T(8,128)(2,1)S(1)}, u32[]{:S(2)}, u32[]{:S(2)}) collective-permute-start(bf16[512,512]{1,0:T(8,128)(2,1)S(1)} %collective-permute-done.31.refs_2_), channel_id=1, source_target_pairs={{0,16},{1,17},{2,18},{3,19},{4,20},{5,21},{6,22},{7,23},{8,24},{9,... | collective-permute-start | bytes 1572872 | tf_op jit(solution)/shard_map/ppermute | solution.py:79
  287.1 23.4 %collective-permute-start.29 = (bf16[512,512]{1,0:T(8,128)(2,1)S(1)}, bf16[512,512]{1,0:T(8,128)(2,1)S(1)}, u32[]{:S(2)}, u32[]{:S(2)}) collective-permute-start(bf16[512,512]{1,0:T(8,128)(2,1)S(1)} %collective-permute-done.28.refs_4_), channel_id=1, source_target_pairs={{0,16},{1,17},{2,18},{3,19},{4,20},{5,21},{6,22},{7,23},{8,24},{9,... | collective-permute-start | bytes 1572872 | tf_op jit(solution)/shard_map/ppermute | solution.py:79
  287.1 23.4 %collective-permute-start.35 = (bf16[512,512]{1,0:T(8,128)(2,1)S(1)}, bf16[512,512]{1,0:T(8,128)(2,1)S(1)}, u32[]{:S(2)}, u32[]{:S(2)}) collective-permute-start(bf16[512,512]{1,0:T(8,128)(2,1)S(1)} %collective-permute-done.31.refs_2_), channel_id=1, source_target_pairs={{0,8},{1,9},{2,10},{3,11},{4,12},{5,13},{6,14},{7,15},{8,0},{9,1},... | collective-permute-start | bytes 1572872 | tf_op jit(solution)/shard_map/ppermute | solution.py:79
  299.8 13.5 %collective-permute-start.33 = (bf16[512,512]{1,0:T(8,128)(2,1)S(1)}, bf16[512,512]{1,0:T(8,128)(2,1)S(1)}, u32[]{:S(2)}, u32[]{:S(2)}) collective-permute-start(bf16[512,512]{1,0:T(8,128)(2,1)S(1)} %collective-permute-done.32.refs_0_), channel_id=1, source_target_pairs={{0,8},{1,9},{2,10},{3,11},{4,12},{5,13},{6,14},{7,15},{8,0},{9,1},... | collective-permute-start | bytes 1572872 | tf_op jit(solution)/shard_map/ppermute | solution.py:79
  310.5 3.8 %collective-permute-start.30 = (bf16[512,512]{1,0:T(8,128)(2,1)S(1)}, bf16[512,512]{1,0:T(8,128)(2,1)S(1)}, u32[]{:S(2)}, u32[]{:S(2)}) collective-permute-start(bf16[512,512]{1,0:T(8,128)(2,1)S(1)} %collective-permute-done.29.refs_0_), channel_id=1, source_target_pairs={{0,8},{1,9},{2,10},{3,11},{4,12},{5,13},{6,14},{7,15},{8,0},{9,1},... | collective-permute-start | bytes 1572872 | tf_op jit(solution)/shard_map/ppermute | solution.py:79
  (12 other events, 32.5 us)
